TPU v7x, 16 devices: a whole 2x2x2 slice. The times are simulated.
16 devices in a mesh: fsdp: 16 (over z, y, x, core).
Axes of the slice: x: 2, y: 2, z: 2, core: 2. Of those that a mesh axis runs over, the one named last changes fastest.
Arguments:
- hidden: bfloat16 [16384, 1152], P('fsdp')
- targets: int32 [16384], P('fsdp')
- resp_mask: int32 [16384], P('fsdp')
- resp_id: int32 [16384], P('fsdp')
- old_logp: float32 [16384], P('fsdp')
- ref_logp: float32 [16384], P('fsdp')
- rewards: float32 [128], P('fsdp')
- prompt_id: int32 [128], P('fsdp')
- norm_w: bfloat16 [1152], P('fsdp')
- embedding: bfloat16 [32000, 1152], P('fsdp')
Outputs:
- output 1: float32 [], replicated
- output 2: bfloat16 [16384, 1152], P('fsdp')
- output 3: float32 [32000, 1152], P('fsdp')
- output 4: float32 [1152], P('fsdp')
All inputs are finite; a program needn't handle non-finite values.
Results may differ from a plain program's by a relative error of at most 0.00129.
Values are sent between devices in bfloat16 or wider.
A program may use at most 1 GiB of HBM per device.

v0:
```python
import jax
import jax.numpy as jnp
from jax import lax
from jax.sharding import PartitionSpec as P

GROUP_SIZE = 8
CLIP_LOW = 0.8
CLIP_HIGH = 1.28
KL_COEF = 0.04
EPSILON = 1e-6
MAX_BLOCK = 256


def token_terms(tok_logp, old_block, ref_block, adv_block):
    ratio = jnp.exp(tok_logp - old_block)
    surr_raw = ratio * adv_block
    surr_clip = jnp.clip(ratio, CLIP_LOW, CLIP_HIGH) * adv_block
    kl_gap = ref_block - tok_logp
    tok_loss = -jnp.minimum(surr_raw, surr_clip) + KL_COEF * (jnp.exp(kl_gap) - kl_gap - 1.0)
    keep = (surr_raw <= surr_clip) | ((ratio > CLIP_LOW) & (ratio < CLIP_HIGH))
    d_logp = -jnp.where(keep, surr_raw, 0.0) + KL_COEF * (1.0 - jnp.exp(kl_gap))
    return tok_loss, d_logp


def solution(mesh):
    shards = mesh.shape['fsdp']

    def local(hidden, targets, resp_mask, resp_id, old_logp, ref_logp, rewards, prompt_id, norm_w, embedding):
        tok_dev, model_dim = hidden.shape
        prompts = rewards.shape[0] * shards // GROUP_SIZE
        emb_full = lax.all_gather(embedding, 'fsdp', tiled=True)
        gain = lax.all_gather(norm_w, 'fsdp', tiled=True).astype(jnp.float32)
        rew_stats = jnp.stack([rewards, rewards * rewards, jnp.ones_like(rewards)], axis=1)
        totals = lax.psum(jax.ops.segment_sum(rew_stats, prompt_id, num_segments=prompts), 'fsdp')
        mask_f = resp_mask.astype(jnp.float32)
        count = lax.psum(jnp.sum(mask_f), 'fsdp')
        mean_r = totals[:, 0] / totals[:, 2]
        std_r = jnp.sqrt(jnp.maximum(totals[:, 1] / totals[:, 2] - mean_r * mean_r, 0.0))
        adv_resp = (rewards - mean_r[prompt_id]) / (std_r[prompt_id] + EPSILON)
        adv_tok = adv_resp[resp_id]
        hid_f32 = hidden.astype(jnp.float32)
        inv_rms = lax.rsqrt(jnp.mean(hid_f32 * hid_f32, axis=-1, keepdims=True) + EPSILON)
        normed = hid_f32 * inv_rms
        x_rows = (normed * gain).astype(jnp.bfloat16)
        vocab_ids = jnp.arange(emb_full.shape[0], dtype=jnp.int32)
        block_len = min(tok_dev, MAX_BLOCK)
        n_blocks = tok_dev // block_len

        def step(grad_emb, pack):
            x_block, tgt_block, mask_block, old_block, ref_block, adv_block = pack
            logits = lax.dot_general(x_block, emb_full, (((1,), (1,)), ((), ())), preferred_element_type=jnp.float32)
            row_max = jnp.max(logits, axis=1, keepdims=True)
            shifted = jnp.exp(logits - row_max)
            sum_exp = jnp.sum(shifted, axis=1, keepdims=True)
            is_target = vocab_ids[None, :] == tgt_block[:, None]
            tok_logp = jnp.sum(jnp.where(is_target, logits, 0.0), axis=1) - (row_max + jnp.log(sum_exp))[:, 0]
            tok_loss, d_logp = token_terms(tok_logp, old_block, ref_block, adv_block)
            tok_coef = (mask_block * d_logp / count)[:, None]
            d_logits = (tok_coef * (jnp.where(is_target, 1.0, 0.0) - shifted / sum_exp)).astype(jnp.bfloat16)
            dx_block = jnp.dot(d_logits, emb_full, preferred_element_type=jnp.float32)
            grad_emb = grad_emb + lax.dot_general(d_logits, x_block, (((0,), (0,)), ((), ())), preferred_element_type=jnp.float32)
            return grad_emb, (jnp.sum(mask_block * tok_loss), dx_block)

        pack = (x_rows.reshape(n_blocks, block_len, model_dim), targets.reshape(n_blocks, block_len), mask_f.reshape(n_blocks, block_len), old_logp.reshape(n_blocks, block_len), ref_logp.reshape(n_blocks, block_len), adv_tok.reshape(n_blocks, block_len))
        grad_full, (loss_parts, dx_blocks) = lax.scan(step, jnp.zeros(emb_full.shape, jnp.float32), pack)
        d_embedding = lax.psum_scatter(grad_full, 'fsdp', scatter_dimension=0, tiled=True)
        d_x = dx_blocks.reshape(tok_dev, model_dim)
        d_norm_w = lax.psum_scatter(jnp.sum(d_x * normed, axis=0), 'fsdp', scatter_dimension=0, tiled=True)
        d_normed = d_x * gain
        d_hidden = (inv_rms * (d_normed - normed * jnp.mean(d_normed * normed, axis=-1, keepdims=True))).astype(jnp.bfloat16)
        mean_loss = lax.psum(jnp.sum(loss_parts), 'fsdp') / count
        return mean_loss, d_hidden, d_embedding, d_norm_w

    tok_spec = P('fsdp')
    row_spec = P('fsdp', None)
    return jax.shard_map(local, mesh=mesh, in_specs=(row_spec, tok_spec, tok_spec, tok_spec, tok_spec, tok_spec, tok_spec, tok_spec, tok_spec, row_spec), out_specs=(P(), row_spec, row_spec, tok_spec), check_vma=False)
```

profile of v0, /device:TPU:0, one launch (start us, length us, event | category | flops | bytes accessed | tf_op | source)
XLA Modules:
  0.0 1742.1 jit_solution(16599970371915298398)
XLA Ops:
  12.2 35.5 %all-reduce.4 = (f32[16,3]{1,0:T(8,128)S(1)}, f32[]{:T(128)}) all-reduce(f32[16,3]{1,0:T(8,128)S(1)} %scatter_custom_fusion, f32[]{:T(128)} %convert_reduce_fusion), channel_id=1, replica_groups=mesh['fsdp'=16] {'fsdp'}, use_global_device_ids=true, to_apply=%region_2.0 | all-reduce | flops 49 | bytes 392 | tf_op jit(solution)/shard_map/psum | solution.py:34
  51.2 5.8 select_select_fusion
  58.5 33.9 %all-reduce = bf16[1152]{0:T(1024)(128)(2,1)S(1)} all-reduce(bf16[1152]{0:T(1024)(128)(2,1)S(1)} %dynamic-update-slice), channel_id=1, replica_groups=mesh['fsdp'=16] {'fsdp'}, use_global_device_ids=true, to_apply=%add | all-reduce | flops 1152 | bytes 4608
  101.9 176.9 %all-gather.2.cloned.1.call-done = bf16[32000,1152]{1,0:T(8,128)(2,1)} async-done(((bf16[2000,1152]{1,0:T(8,128)(2,1)}), bf16[32000,1152]{1,0:T(8,128)(2,1)}) %all-gather.2.cloned.1.call-update) | async-done | bytes 73728016 | tf_op jit(solution)/shard_map/all_gather | solution.py:31
  278.7 780.2 %while.17 = (s32[]{:T(128)}, f32[32000,1152]{1,0:T(8,128)}, f32[4]{0:T(128)}, f32[4,256,1152]{2,1,0:T(8,128)}, f32[4,256]{1,0:T(4,128)}, /*index=5*/s32[4,256]{1...) while((s32[]{:T(128)}, f32[32000,1152]{1,0:T(8,128)}, ...), condition=%wide.region_10.11_spmd.clone, body=%wide.region_5.10_spmd.clone.sunk | while | flops 56860680192 | bytes 575831936 | solution.py:65
  278.8 39.3 %fusion.67 = (f32[256]{0:T(256)S(1)}, f32[256,32000]{1,0:T(8,128)}) fusion(bf16[32000,1152]{1,0:T(8,128)(2,1)} %get-tuple-element.389, bf16[4,256,1152]{2,1,0:T(8,128)(2,1)S(1)} %get-tuple-element.388, s32[]{:T(128)} %get-tuple-element.368), kind=kOutput, calls=%fused_computation.74.clone.1 | convolution fusion | flops 18882560000 | bytes 107086848 | tf_op jit(solution)/shard_map/while/body/eval_jaxpr/dot_general | solution.py:51
  318.7 16.2 fusion.68
  337.5 62.4 %convolution_add_fusion.2 = f32[32000,1152]{1,0:T(8,128)} fusion(f32[32000,1152]{1,0:T(8,128)} %get-tuple-element.369, pred[]{:T(512)S(6)} %compare.18, bf16[4,256,1152]{2,1,0:T(8,128)(2,1)S(1)} %get-tuple-element.388, s32[]{:T(128)} %get-tuple-element.368, f32[256,32000]{1,0:T(8,128)} %get-tuple-element.344, f32[256]{0:T(256)S(1)} %get-tuple-element.346, ...), kind=kOutput, calls=%fused_computation.4.clone.3 | convolution fusion | flops 19005440000 | bytes 328273920 | tf_op jit(solution)/shard_map/while/body/eval_jaxpr/dot_general | solution.py:61
  399.9 37.9 %fusion.70 = f32[4,256,1152]{2,1,0:T(8,128)} fusion(f32[4,256,1152]{2,1,0:T(8,128)} %get-tuple-element.371, s32[]{:T(128)} %get-tuple-element.368, bf16[32000,1152]{1,0:T(8,128)(2,1)} %get-tuple-element.389, f32[256,32000]{1,0:T(8,128)} %get-tuple-element.344, f32[256]{0:T(256)S(1)} %get-tuple-element.346, f32[256]{0:T(256)S(1)} %get-tuple-element.352, ...), kind=kOutput, calls=%fused_computation.15.clone.1 | convolution fusion | flops 18931712000 | bytes 107680256 | tf_op jit(solution)/shard_map/while/body/eval_jaxpr/dot_general | solution.py:60
  439.0 39.3 %fusion.67 = (f32[256]{0:T(256)S(1)}, f32[256,32000]{1,0:T(8,128)}) fusion(bf16[32000,1152]{1,0:T(8,128)(2,1)} %get-tuple-element.389, bf16[4,256,1152]{2,1,0:T(8,128)(2,1)S(1)} %get-tuple-element.388, s32[]{:T(128)} %get-tuple-element.368), kind=kOutput, calls=%fused_computation.74.clone.1 | convolution fusion | flops 18882560000 | bytes 107086848 | tf_op jit(solution)/shard_map/while/body/eval_jaxpr/dot_general | solution.py:51
  479.0 16.2 fusion.68
  497.8 108.8 %convolution_add_fusion.2 = f32[32000,1152]{1,0:T(8,128)} fusion(f32[32000,1152]{1,0:T(8,128)} %get-tuple-element.369, pred[]{:T(512)S(6)} %compare.18, bf16[4,256,1152]{2,1,0:T(8,128)(2,1)S(1)} %get-tuple-element.388, s32[]{:T(128)} %get-tuple-element.368, f32[256,32000]{1,0:T(8,128)} %get-tuple-element.344, f32[256]{0:T(256)S(1)} %get-tuple-element.346, ...), kind=kOutput, calls=%fused_computation.4.clone.3 | convolution fusion | flops 19005440000 | bytes 328273920 | tf_op jit(solution)/shard_map/while/body/eval_jaxpr/dot_general | solution.py:61
  606.6 37.9 %fusion.70 = f32[4,256,1152]{2,1,0:T(8,128)} fusion(f32[4,256,1152]{2,1,0:T(8,128)} %get-tuple-element.371, s32[]{:T(128)} %get-tuple-element.368, bf16[32000,1152]{1,0:T(8,128)(2,1)} %get-tuple-element.389, f32[256,32000]{1,0:T(8,128)} %get-tuple-element.344, f32[256]{0:T(256)S(1)} %get-tuple-element.346, f32[256]{0:T(256)S(1)} %get-tuple-element.352, ...), kind=kOutput, calls=%fused_computation.15.clone.1 | convolution fusion | flops 18931712000 | bytes 107680256 | tf_op jit(solution)/shard_map/while/body/eval_jaxpr/dot_general | solution.py:60
  645.7 39.3 %fusion.67 = (f32[256]{0:T(256)S(1)}, f32[256,32000]{1,0:T(8,128)}) fusion(bf16[32000,1152]{1,0:T(8,128)(2,1)} %get-tuple-element.389, bf16[4,256,1152]{2,1,0:T(8,128)(2,1)S(1)} %get-tuple-element.388, s32[]{:T(128)} %get-tuple-element.368), kind=kOutput, calls=%fused_computation.74.clone.1 | convolution fusion | flops 18882560000 | bytes 107086848 | tf_op jit(solution)/shard_map/while/body/eval_jaxpr/dot_general | solution.py:51
  685.6 16.2 fusion.68
  704.5 108.8 %convolution_add_fusion.2 = f32[32000,1152]{1,0:T(8,128)} fusion(f32[32000,1152]{1,0:T(8,128)} %get-tuple-element.369, pred[]{:T(512)S(6)} %compare.18, bf16[4,256,1152]{2,1,0:T(8,128)(2,1)S(1)} %get-tuple-element.388, s32[]{:T(128)} %get-tuple-element.368, f32[256,32000]{1,0:T(8,128)} %get-tuple-element.344, f32[256]{0:T(256)S(1)} %get-tuple-element.346, ...), kind=kOutput, calls=%fused_computation.4.clone.3 | convolution fusion | flops 19005440000 | bytes 328273920 | tf_op jit(solution)/shard_map/while/body/eval_jaxpr/dot_general | solution.py:61
  813.2 37.9 %fusion.70 = f32[4,256,1152]{2,1,0:T(8,128)} fusion(f32[4,256,1152]{2,1,0:T(8,128)} %get-tuple-element.371, s32[]{:T(128)} %get-tuple-element.368, bf16[32000,1152]{1,0:T(8,128)(2,1)} %get-tuple-element.389, f32[256,32000]{1,0:T(8,128)} %get-tuple-element.344, f32[256]{0:T(256)S(1)} %get-tuple-element.346, f32[256]{0:T(256)S(1)} %get-tuple-element.352, ...), kind=kOutput, calls=%fused_computation.15.clone.1 | convolution fusion | flops 18931712000 | bytes 107680256 | tf_op jit(solution)/shard_map/while/body/eval_jaxpr/dot_general | solution.py:60
  852.3 39.3 %fusion.67 = (f32[256]{0:T(256)S(1)}, f32[256,32000]{1,0:T(8,128)}) fusion(bf16[32000,1152]{1,0:T(8,128)(2,1)} %get-tuple-element.389, bf16[4,256,1152]{2,1,0:T(8,128)(2,1)S(1)} %get-tuple-element.388, s32[]{:T(128)} %get-tuple-element.368), kind=kOutput, calls=%fused_computation.74.clone.1 | convolution fusion | flops 18882560000 | bytes 107086848 | tf_op jit(solution)/shard_map/while/body/eval_jaxpr/dot_general | solution.py:51
  892.3 16.2 fusion.68
  911.1 108.8 %convolution_add_fusion.2 = f32[32000,1152]{1,0:T(8,128)} fusion(f32[32000,1152]{1,0:T(8,128)} %get-tuple-element.369, pred[]{:T(512)S(6)} %compare.18, bf16[4,256,1152]{2,1,0:T(8,128)(2,1)S(1)} %get-tuple-element.388, s32[]{:T(128)} %get-tuple-element.368, f32[256,32000]{1,0:T(8,128)} %get-tuple-element.344, f32[256]{0:T(256)S(1)} %get-tuple-element.346, ...), kind=kOutput, calls=%fused_computation.4.clone.3 | convolution fusion | flops 19005440000 | bytes 328273920 | tf_op jit(solution)/shard_map/while/body/eval_jaxpr/dot_general | solution.py:61
  1019.9 37.9 %fusion.70 = f32[4,256,1152]{2,1,0:T(8,128)} fusion(f32[4,256,1152]{2,1,0:T(8,128)} %get-tuple-element.371, s32[]{:T(128)} %get-tuple-element.368, bf16[32000,1152]{1,0:T(8,128)(2,1)} %get-tuple-element.389, f32[256,32000]{1,0:T(8,128)} %get-tuple-element.344, f32[256]{0:T(256)S(1)} %get-tuple-element.346, f32[256]{0:T(256)S(1)} %get-tuple-element.352, ...), kind=kOutput, calls=%fused_computation.15.clone.1 | convolution fusion | flops 18931712000 | bytes 107680256 | tf_op jit(solution)/shard_map/while/body/eval_jaxpr/dot_general | solution.py:60
  1064.2 32.1 %all-reduce.3 = (f32[]{:T(128)}, f32[1152]{0:T(1024)S(1)}) all-reduce(f32[]{:T(128)} %reduce_sum.83, f32[1152]{0:T(1024)S(1)} %get-tuple-element.213), channel_id=1, replica_groups=mesh['fsdp'=16] {'fsdp'}, use_global_device_ids=true, to_apply=%region_12.13 | all-reduce | flops 1153 | bytes 9224 | tf_op jit(solution)/shard_map/psum | solution.py:71
  1098.2 4.0 fusion.36
  1102.2 631.9 %reduce-scatter.4.cloned.1.call-done = f32[2000,1152]{1,0:T(8,128)} async-done(((f32[32000,1152]{1,0:T(8,128)}), f32[2000,1152]{1,0:T(8,128)}) %reduce-scatter.4.cloned.1.call-update) | async-done | bytes 9216016
  (85 shorter events, 43.4 us)
Async XLA Ops:
  7.2 271.6 %all-gather.2.cloned.1.call-start = ((), (), s32[]{:S(2)}) async-start(), calls=%async_computation.1 | async-start | bytes 78336000 | tf_op jit(solution)/shard_map/all_gather | solution.py:31
  7.9 1726.3 %reduce-scatter.4.cloned.1.call-start = ((), (), s32[]{:S(2)}) async-start(), calls=%async_computation.2 | async-start | bytes 156672000
  92.3 186.4 %copy-start.1 = (f32[1152]{0:T(1024)}, f32[1152]{0:T(1024)S(1)}, u32[]{:S(2)}) copy-start(f32[1152]{0:T(1024)S(1)} %convert_element_type.23) | copy-start | bytes 13828
  99.0 0.6 copy-start.3
  399.9 37.9 %copy-start.5 = (f32[4]{0:T(128)S(1)}, f32[4]{0:T(128)}, u32[]{:S(2)}) copy-start(f32[4]{0:T(128)} %get-tuple-element.370) | copy-start | bytes 52 | tf_op jit(solution)/shard_map/while
  438.5 0.5 copy-start.6
  606.6 37.9 %copy-start.5 = (f32[4]{0:T(128)S(1)}, f32[4]{0:T(128)}, u32[]{:S(2)}) copy-start(f32[4]{0:T(128)} %get-tuple-element.370) | copy-start | bytes 52 | tf_op jit(solution)/shard_map/while
  645.2 0.5 copy-start.6
  813.2 37.9 %copy-start.5 = (f32[4]{0:T(128)S(1)}, f32[4]{0:T(128)}, u32[]{:S(2)}) copy-start(f32[4]{0:T(128)} %get-tuple-element.370) | copy-start | bytes 52 | tf_op jit(solution)/shard_map/while
  851.8 0.5 copy-start.6
  1019.9 37.9 %copy-start.5 = (f32[4]{0:T(128)S(1)}, f32[4]{0:T(128)}, u32[]{:S(2)}) copy-start(f32[4]{0:T(128)} %get-tuple-element.370) | copy-start | bytes 52 | tf_op jit(solution)/shard_map/while
  1058.4 0.5 copy-start.6
  1058.9 0.7 copy-start.7
  1058.9 1.7 copy-start
  1058.9 1.7 copy-start.2
  1058.9 1.7 copy-start.4
Sparse Core Ops, SparseCore 0:
  10.2 268.4 all-gather.1
  1059.1 675.0 reduce-scatter.3
where the time goes:
time: 1740 us
  waiting for transfers between devices  810 us (47%)
  matrix products  697 us (40%)
  blocking collectives  101 us (6%)
  other arithmetic  93.7 us (5%)
  local copies, waits for them, and re-layouts  23.3 us (1%)
    unnamed x3, waiting for transfers between devices  633 us
    dot_general x4, matrix products, step(): lax.dot_general(d_logits, x_block, (((0,), (0,)), ((), ())), preferred_el...  389 us
    all_gather x1, waiting for transfers between devices, local(): emb_full = lax.all_gather(embedding, 'fsdp', tiled=True)  177 us
    dot_general x4, matrix products, step(): lax.dot_general(x_block, emb_full, (((1,), (1,)), ((), ())), preferred_el...  157 us
    dot_general x4, matrix products, step(): dx_block = jnp.dot(d_logits, emb_full, preferred_element_type=jnp.float32)  151 us
    reduce_sum x4, other arithmetic, step(): jnp.sum(jnp.where(is_target, logits, 0.0), axis=1)  64.7 us
    psum x1, blocking collectives, local(): lax.psum(jax.ops.segment_sum(rew_stats, prompt_id, num_segments=prompts),...  35.5 us
  transfers between devices with their start and end apart: 2, of which 2 were waited for; matrix products, arithmetic and copies ran while one was open for 2% of the time, Pallas kernels for 0%

commit v1 on v0

v1 whole, which is shorter than its diff:
```python
import functools

import jax
import jax.numpy as jnp
from jax import lax
from jax.experimental import pallas as pl
from jax.experimental.pallas import tpu as pltpu
from jax.sharding import PartitionSpec as P


GROUP_SIZE = 8
CLIP_LOW = 0.8
CLIP_HIGH = 1.28
KL_COEF = 0.04
EPSILON = 1e-6
CHUNKS = 4
GROUP = 2
BF16 = jnp.bfloat16
F32 = jnp.float32
RELATIVE = (0, 2, 4, 6, 1, 3, 5, 7)
PARAMS = pltpu.CompilerParams(vmem_limit_bytes=62 * 1024 * 1024)
ANY = pl.BlockSpec(memory_space=pl.ANY)
LIST = 32
SLOTS = 2
BOTH_LAST = (((1,), (1,)), ((), ()))
PIECE = 256
N_LISTS = 11
ACTIVE = N_LISTS * LIST
COUNTS = ACTIVE + LIST
PLACE = COUNTS + N_LISTS
FIRST = PLACE + 8


def token_terms(tok_logp, old_block, ref_block, adv_block):
    ratio = jnp.exp(tok_logp - old_block)
    surr_raw = ratio * adv_block
    surr_clip = jnp.clip(ratio, CLIP_LOW, CLIP_HIGH) * adv_block
    kl_gap = ref_block - tok_logp
    tok_loss = -jnp.minimum(surr_raw, surr_clip) + KL_COEF * (jnp.exp(kl_gap) - kl_gap - 1.0)
    keep = (surr_raw <= surr_clip) | ((ratio > CLIP_LOW) & (ratio < CLIP_HIGH))
    d_logp = -jnp.where(keep, surr_raw, 0.0) + KL_COEF * (1.0 - jnp.exp(kl_gap))
    return tok_loss, d_logp


def corner(*_):
    return 0, 0


def row_ids(cols):
    return lax.broadcasted_iota(jnp.int32, (8, cols), 0)


def logits_call(tab, which, emb, x_all, tgt, prev, order, row, first_block, blocks, wide, hid=None, gain8=None):
    rows, dim = emb.shape
    total = tgt.shape[1]
    make = hid is not None
    at = lambda i, t: t[row * LIST + i]

    def body(tab_ref, emb_ref, tgt_ref, src_ref, *refs):
        z_ref, stat_ref = refs[-2:]

        @pl.when(pl.program_id(0) < tab_ref[COUNTS + row])
        def _():
            x_ref = src_ref
            if make:
                x_ref = refs[-3]
                gain = refs[0][pl.ds(0, 1), :]
                for r in range(0, wide, 32):
                    hid = src_ref[pl.ds(r, 32), :].astype(F32)
                    inv = lax.rsqrt(jnp.mean(hid * hid, axis=-1, keepdims=True) + EPSILON)
                    x_ref[pl.ds(r, 32), :] = (hid * inv * gain).astype(BF16)
            rel = tgt_ref[pl.ds(0, 1), :] - tab_ref[FIRST + which]
            ids = row_ids(wide)
            tops, tots, hits = [], [], []
            for a in range(0, rows, 400):
                sub = 400
                z_ref[pl.ds(a, sub), :] = lax.dot_general(emb_ref[pl.ds(a, sub), :], x_ref[...], BOTH_LAST, preferred_element_type=F32)
                top = z_ref[pl.ds(a, 8), :]
                for r in range(a, a + sub, 8):
                    top = jnp.maximum(top, z_ref[pl.ds(r, 8), :])
                tot = jnp.zeros((8, wide), F32)
                hit = jnp.zeros((8, wide), F32)
                for r in range(a, a + sub, 8):
                    z = z_ref[pl.ds(r, 8), :]
                    tot = tot + jnp.exp(z - top)
                    hit = hit + jnp.where(ids == rel - r, z, 0.0)
                tops.append(top)
                tots.append(tot)
                hits.append(hit)
            top = jnp.max(functools.reduce(jnp.maximum, tops), axis=0, keepdims=True)
            tot = sum(t * jnp.exp(m - top) for m, t in zip(tops, tots))
            down = lambda v: jnp.sum(v, axis=0, keepdims=True)
            stat_ref[...] = jnp.concatenate([top, down(tot), down(sum(hits)), jnp.zeros((5, wide), F32)], axis=0)

    in_specs = [
        pl.BlockSpec((rows, dim), corner, pipeline_mode=pl.Buffered(1)),
        pl.BlockSpec((8, wide), lambda i, t: (0, at(i, t))),
        pl.BlockSpec((wide, dim), lambda i, t: ((t[PLACE + at(i, t) - first_block] if make else at(i, t)), 0)),
    ]
    args = [tab, emb, tgt, hid if make else x_all]
    out_shape = [jax.ShapeDtypeStruct((rows, total), F32), jax.ShapeDtypeStruct((8, blocks * wide), F32)]
    out_specs = [pl.BlockSpec((rows, wide), lambda i, t: (0, at(i, t))), pl.BlockSpec((8, wide), lambda i, t: (0, at(i, t) - first_block))]
    if make:
        in_specs.append(pl.BlockSpec((8, dim), corner))
        args.append(gain8)
        out_shape.insert(0, jax.ShapeDtypeStruct((total, dim), BF16))
        out_specs.insert(0, pl.BlockSpec((wide, dim), lambda i, t: (at(i, t), 0)))
    in_specs.append(ANY)
    args.append(order)
    alias = {len(args) + j: j for j in range(len(prev))}
    return pl.pallas_call(
        body,
        out_shape=out_shape,
        grid_spec=pltpu.PrefetchScalarGridSpec(num_scalar_prefetch=1, grid=(blocks,), in_specs=in_specs + [ANY] * len(prev), out_specs=out_specs),
        input_output_aliases=alias,
        compiler_params=PARAMS,
        name='logits',
    )(*args, *prev)


def grad_rows(z_ref, out_ref, base, col, a, n, meta, rel):
    lse, coef = meta[0:1], meta[1:2]
    wide = meta.shape[1]
    ids = row_ids(wide)
    for r in range(a, a + n, 8):
        prob = jnp.exp(z_ref[pl.ds(r, 8), :] - lse)
        grad = coef * (jnp.where(ids == rel - r, 1.0, 0.0) - prob)
        out_ref[pl.ds(base + r, 8), pl.ds(col, wide)] = grad.astype(BF16)


def dx_call(tab, z_own, z_par, turned_own, turned_par, meta, order, row, first_block, blocks, wide, begin=None):
    rows, _ = z_own.shape
    dim, padded = turned_own.shape
    half = dim // 2
    sub = 256
    keep = begin is not None
    at = lambda i, t: t[row * LIST + i]

    def body(tab_ref, zo_ref, zp_ref, eto_ref, etp_ref, meta_ref, *refs):
        dz_ref, acc_ref = refs[-2:]
        step = pl.program_id(0)
        place = step % 4
        block = first_block + (step // 4) * 8 + place

        @pl.when(tab_ref[ACTIVE + block] > 0)
        def _():
            meta = meta_ref[...]
            tgt = meta[2:3].astype(jnp.int32)
            for h, (z_ref, et_ref) in enumerate(((zo_ref, eto_ref), (zp_ref, etp_ref))):
                dz_ref[pl.ds(h * padded + rows, padded - rows), :] = jnp.zeros((padded - rows, wide), BF16)
                for a in range(0, padded, sub):
                    grad_rows(z_ref, dz_ref, h * padded, 0, a, min(sub, rows - a), meta, tgt - tab_ref[FIRST + h])
                    part = jnp.dot(et_ref[:, pl.ds(a, sub)], dz_ref[pl.ds(h * padded + a, sub), :], preferred_element_type=F32)
                    acc_ref[...] = part if h + a == 0 else acc_ref[...] + part

        @pl.when(tab_ref[ACTIVE + block] == 0)
        def _():
            acc_ref[...] = jnp.zeros_like(acc_ref)

        if not keep:
            refs[1][0] = acc_ref[...]
            return
        start_ref, keep_a, send_a, keep_b, send_b = refs[1:6]
        for q in range(4):

            @pl.when(place == q)
            def _():
                (send_a if q % 2 else keep_a)[0] = acc_ref[pl.ds(0, half), :] + start_ref[0, pl.ds(0, half), :]
                (send_b if q // 2 else keep_b)[q % 2] = acc_ref[pl.ds(half, half), :] + start_ref[0, pl.ds(half, half), :]

    in_specs = [
        pl.BlockSpec((rows, wide), lambda i, t: (0, at(i, t))),
        pl.BlockSpec((rows, wide), lambda i, t: (0, at(i, t))),
        pl.BlockSpec((dim, padded), corner, pipeline_mode=pl.Buffered(1)),
        pl.BlockSpec((dim, padded), corner, pipeline_mode=pl.Buffered(1)),
        pl.BlockSpec((8, wide), lambda i, t: (0, at(i, t))),
        ANY,
    ]
    args = [tab, z_own, z_par, turned_own, turned_par, meta, order]
    one = pl.BlockSpec((1, dim, wide), lambda i, t: (i, 0, 0))
    if keep:
        in_specs.append(one)
        args.append(begin)
        out_shape = [jax.ShapeDtypeStruct((blocks // 2, half, wide), F32)] * 4
        by_place = pl.BlockSpec((1, half, wide), lambda i, t: (i // 2, 0, 0))
        by_chunk = pl.BlockSpec((2, half, wide), lambda i, t: (i // 4, 0, 0))
        out_specs = [by_place, by_place, by_chunk, by_chunk]
    else:
        out_shape = jax.ShapeDtypeStruct((blocks, dim, wide), F32)
        out_specs = one
    return pl.pallas_call(
        body,
        out_shape=out_shape,
        grid_spec=pltpu.PrefetchScalarGridSpec(
            num_scalar_prefetch=1,
            grid=(blocks,),
            in_specs=in_specs,
            out_specs=out_specs,
            scratch_shapes=[pltpu.VMEM((2 * padded, wide), BF16), pltpu.VMEM((dim, wide), F32)],
        ),
        compiler_params=PARAMS,
        name='dx',
    )(*args)


def de_call(tab, which, z, x_all, meta, order, row, part, n_parts, wide, begin=None, into=None):
    rows_all, total = z.shape
    rows = rows_all // n_parts
    dim = x_all.shape[1]
    at = lambda j: (lambda i, t: t[row * LIST + i * SLOTS + j])

    def body(tab_ref, *refs):
        z_refs, x_refs, meta_refs = refs[:SLOTS], refs[SLOTS:2 * SLOTS], refs[2 * SLOTS:3 * SLOTS]
        out_ref, dz_ref, rows_ref = refs[-3:]
        step = pl.program_id(0)

        @pl.when(step == 0)
        def _():
            out_ref[...] = jnp.zeros_like(out_ref) if begin is None else refs[3 * SLOTS + 1][...]

        @pl.when(step * SLOTS < tab_ref[COUNTS + row])
        def _():
            metas, rels = [], []
            for j in range(SLOTS):
                meta = meta_refs[j][...]
                live = jnp.where(step * SLOTS + j < tab_ref[COUNTS + row], 1.0, 0.0)
                rels.append(meta[2:3].astype(jnp.int32) - tab_ref[FIRST + which] - part * rows)
                metas.append(jnp.concatenate([meta[0:1], meta[1:2] * live], axis=0))
                rows_ref[pl.ds(j * wide, wide), :] = x_refs[j][...]
            for a in range(0, rows, PIECE):
                n = min(PIECE, rows - a)
                for j in range(SLOTS):
                    grad_rows(z_refs[j], dz_ref, 0, j * wide, a, n, metas[j], rels[j])
                out_ref[pl.ds(a, n), :] += jnp.dot(dz_ref[pl.ds(a, n), :], rows_ref[...], preferred_element_type=F32)

    maps = [at(j) for j in range(SLOTS)]
    in_specs = [pl.BlockSpec((rows, wide), lambda i, t, m=m: (part, m(i, t))) for m in maps]
    in_specs += [pl.BlockSpec((wide, dim), lambda i, t, m=m: (m(i, t), 0)) for m in maps]
    in_specs += [pl.BlockSpec((8, wide), lambda i, t, m=m: (0, m(i, t))) for m in maps] + [ANY]
    order = meta if order is into else order
    args = [tab] + [z] * SLOTS + [x_all] * SLOTS + [meta] * SLOTS + [order]
    alias = {}
    whole = begin is not None
    if whole:
        in_specs.append(pl.BlockSpec((rows, dim), corner, pipeline_mode=pl.Buffered(1)))
        args.append(begin)
    if into is not None:
        alias = {len(args): 0}
        in_specs.append(ANY)
        args.append(into)
    return pl.pallas_call(
        body,
        out_shape=jax.ShapeDtypeStruct((rows_all if whole else rows, dim), F32),
        grid_spec=pltpu.PrefetchScalarGridSpec(
            num_scalar_prefetch=1,
            grid=(total // wide // SLOTS,),
            in_specs=in_specs,
            out_specs=pl.BlockSpec((rows, dim), lambda i, t: (part if whole else 0, 0)),
            scratch_shapes=[pltpu.VMEM((rows, SLOTS * wide), BF16), pltpu.VMEM((SLOTS * wide, dim), BF16)],
        ),
        input_output_aliases=alias,
        compiler_params=PARAMS,
        name='de',
    )(*args)


def turn_call(emb, order):
    rows, dim = emb.shape
    n = pl.cdiv(rows, 256)

    def body(emb_ref, order_ref, out_ref):
        left = rows - pl.program_id(0) * 256
        row = lax.broadcasted_iota(jnp.int32, emb_ref.shape, 0)
        out_ref[...] = jnp.where(row < left, emb_ref[...], jnp.zeros_like(emb_ref)).T

    return pl.pallas_call(
        body,
        grid=(n,),
        out_shape=jax.ShapeDtypeStruct((dim, n * 256), BF16),
        in_specs=[pl.BlockSpec((256, dim), lambda i: (i, 0)), ANY],
        out_specs=pl.BlockSpec((dim, 256), lambda i: (0, i)),
        compiler_params=PARAMS,
        name='turn',
    )(emb, order)


def flipped(me, mask):
    out = me
    bit = 1
    while bit <= mask:
        if mask & bit:
            out = out + bit - 2 * bit * ((me // bit) % 2)
        bit *= 2
    return out


def share_call(block, shards, ident):
    def body(in_ref, out_ref, send_sem, recv_sem):
        me = lax.axis_index('fsdp')
        peers = [flipped(me, r) for r in range(1, shards)]
        barrier = pltpu.get_barrier_semaphore()
        for peer in peers:
            pl.semaphore_signal(barrier, inc=1, device_id=(peer,), device_id_type=pl.DeviceIdType.MESH)
        pl.semaphore_wait(barrier, shards - 1)
        copies = []
        for r, peer in enumerate(peers):
            copy = pltpu.make_async_remote_copy(src_ref=in_ref, dst_ref=out_ref.at[me], send_sem=send_sem.at[r], recv_sem=recv_sem.at[r], device_id=(peer,), device_id_type=pl.DeviceIdType.MESH)
            copy.start()
            copies.append(copy)
        out_ref[me] = in_ref[...]
        for copy in copies:
            copy.wait()

    return pl.pallas_call(
        body,
        out_shape=jax.ShapeDtypeStruct((shards,) + block.shape, block.dtype),
        in_specs=[pl.BlockSpec(memory_space=pltpu.VMEM)],
        out_specs=pl.BlockSpec(memory_space=pltpu.VMEM),
        scratch_shapes=[pltpu.SemaphoreType.DMA((shards - 1,)), pltpu.SemaphoreType.DMA((shards - 1,))],
        compiler_params=pltpu.CompilerParams(collective_id=ident, has_side_effects=True),
        name='share',
    )(block)


def coef_call(own_stats, par_stats, token, tgt, team, wide, ident):
    tok_dev = token.shape[1]
    n = tok_dev // wide
    n_own, n_par = len(own_stats), len(par_stats)

    def body(*refs):
        own, par = refs[:n_own], refs[n_own:n_own + n_par]
        token_ref, tgt_ref, meta_ref, loss_ref, out_buf, in_buf, send2, back, send_sem, recv_sem, send_sem2, recv_sem2 = refs[n_own + n_par:]
        me = lax.axis_index('fsdp')
        peers = [flipped(me, r) for r in RELATIVE[1:]]
        for ref in (out_buf, send2, meta_ref):
            ref[...] = jnp.zeros_like(ref)
        for k in range(n):
            a = own[k * n_own // n][:, pl.ds(k % (n // n_own) * team * wide, team * wide)]
            b = par[k * n_par // n][:, pl.ds(k % (n // n_par) * team * wide, team * wide)]
            top = jnp.maximum(a[0:1], b[0:1])
            tot = a[1:2] * jnp.exp(a[0:1] - top) + b[1:2] * jnp.exp(b[0:1] - top)
            hit = a[2:3] + b[2:3]
            for p in range(team):
                at = slice(p * wide, (p + 1) * wide)
                dst = out_buf if p else in_buf
                dst[p, 0:1, pl.ds(k * wide, wide)] = top[:, at]
                dst[p, 1:2, pl.ds(k * wide, wide)] = tot[:, at]
                dst[p, 2:3, pl.ds(k * wide, wide)] = hit[:, at]
        barrier = pltpu.get_barrier_semaphore()
        for peer in peers:
            pl.semaphore_signal(barrier, inc=1, device_id=(peer,), device_id_type=pl.DeviceIdType.MESH)
        pl.semaphore_wait(barrier, team - 1)
        copies = []
        for p in range(1, team):
            copy = pltpu.make_async_remote_copy(src_ref=out_buf.at[p], dst_ref=in_buf.at[p], send_sem=send_sem.at[p], recv_sem=recv_sem.at[p], device_id=(peers[p - 1],), device_id_type=pl.DeviceIdType.MESH)
            copy.start()
            copies.append(copy)
        for copy in copies:
            copy.wait()
        top = in_buf[0, 0:1, :]
        for p in range(1, team):
            top = jnp.maximum(top, in_buf[p, 0:1, :])
        tot = jnp.zeros_like(top)
        hit = jnp.zeros_like(top)
        for p in range(team):
            tot = tot + in_buf[p, 1:2, :] * jnp.exp(in_buf[p, 0:1, :] - top)
            hit = hit + in_buf[p, 2:3, :]
        lse = top + jnp.log(tot)
        mask = token_ref[0:1, :]
        tok_loss, d_logp = token_terms(hit - lse, token_ref[1:2, :], token_ref[2:3, :], token_ref[3:4, :])
        send2[0:1, :] = lse
        send2[1:2, :] = jnp.where(mask > 0.0, d_logp / token_ref[4:5, :], 0.0)
        loss_ref[...] = jnp.broadcast_to(jnp.where(mask > 0.0, tok_loss, 0.0), loss_ref.shape)
        copies = []
        for p in range(1, team):
            copy = pltpu.make_async_remote_copy(src_ref=send2, dst_ref=back.at[p], send_sem=send_sem2.at[p], recv_sem=recv_sem2.at[p], device_id=(peers[p - 1],), device_id_type=pl.DeviceIdType.MESH)
            copy.start()
            copies.append(copy)
        back[0] = send2[...]
        for copy in copies:
            copy.wait()
        for k in range(n):
            for p in range(team):
                at = pl.ds((k * team + p) * wide, wide)
                meta_ref[0:2, at] = back[p, 0:2, pl.ds(k * wide, wide)]
        meta_ref[2:3, :] = tgt_ref[0:1, :].astype(F32)

    vmem = pl.BlockSpec(memory_space=pltpu.VMEM)
    return pl.pallas_call(
        body,
        out_shape=[jax.ShapeDtypeStruct((8, n * team * wide), F32), jax.ShapeDtypeStruct((8, tok_dev), F32)],
        in_specs=[vmem] * (n_own + n_par + 2),
        out_specs=[vmem, vmem],
        scratch_shapes=[pltpu.VMEM((team, 8, tok_dev), F32), pltpu.VMEM((team, 8, tok_dev), F32), pltpu.VMEM((8, tok_dev), F32), pltpu.VMEM((team, 8, tok_dev), F32)] + [pltpu.SemaphoreType.DMA((team,))] * 4,
        compiler_params=pltpu.CompilerParams(collective_id=ident, has_side_effects=True),
        name='coef',
    )(*own_stats, *par_stats, token, tgt)


def second_sum(keep_a, recv_a, keep_b, recv_b, order):
    n, half, wide = keep_a.shape

    def body(ka, ra, kb, rb, order_ref, fa, sa, fb, sb):
        fa[0] = ka[0] + ra[0]
        sa[0] = ka[1] + ra[1]
        fb[0] = kb[0] + rb[0]
        sb[0] = kb[1] + rb[1]

    step = half // 2
    two = pl.BlockSpec((2, step, wide), lambda g, i: (g, i, 0))
    one = pl.BlockSpec((1, step, wide), lambda g, i: (g, i, 0))
    return pl.pallas_call(
        body,
        grid=(n // 2, 2),
        out_shape=[jax.ShapeDtypeStruct((n // 2, half, wide), F32)] * 4,
        in_specs=[two] * 4 + [ANY],
        out_specs=[one] * 4,
        compiler_params=PARAMS,
        name='second_sum',
    )(keep_a, recv_a, keep_b, recv_b, order)


def hidden_kernel(fa_ref, ra_ref, fb_ref, rb_ref, hid_ref, gain_ref, dg_ref):
    d_x = jnp.concatenate([(fa_ref[0] + ra_ref[0]).T, (fb_ref[0] + rb_ref[0]).T], axis=1)
    hid = hid_ref[...].astype(F32)
    inv = lax.rsqrt(jnp.mean(hid * hid, axis=-1, keepdims=True) + EPSILON)
    normed = hid * inv
    dg_ref[...] = jnp.broadcast_to(jnp.sum(d_x * normed, axis=0, keepdims=True), dg_ref.shape)
    d_normed = d_x * gain_ref[0:1, :]
    return (inv * (d_normed - normed * jnp.mean(d_normed * normed, axis=-1, keepdims=True))).astype(BF16)


def hidden_call(parts, hidden, gain8, to_spot, prev, order, k):
    n, half, wide = parts[0].shape
    tokens, dim = hidden.shape

    def body(*refs):
        spot_ref, dh_ref, dg_ref, acc_ref = refs[6], *refs[-3:]
        step = pl.program_id(0)
        rows = hidden_kernel(*refs[:6], dg_ref)
        back = lax.dot_general(spot_ref[...], rows, (((0,), (0,)), ((), ())), preferred_element_type=F32)

        @pl.when(step == 0)
        def _():
            acc_ref[...] = back if prev is None else back + refs[-4][...].astype(F32)

        @pl.when(step > 0)
        def _():
            dh_ref[...] = (acc_ref[...] + back).astype(BF16)

    in_specs = [pl.BlockSpec((1, half, wide), lambda i: (i, 0, 0))] * 4 + [
        pl.BlockSpec((wide, dim), lambda i: (k * n + i, 0)),
        pl.BlockSpec((8, dim), corner),
        pl.BlockSpec((wide, tokens), lambda i: (k * n + i, 0)),
        ANY,
    ]
    args = [*parts, hidden, gain8, to_spot, order]
    if prev is not None:
        in_specs.append(pl.BlockSpec((tokens, dim), corner))
        args.append(prev)
    return pl.pallas_call(
        body,
        grid=(n,),
        out_shape=[jax.ShapeDtypeStruct(hidden.shape, BF16), jax.ShapeDtypeStruct((8 * n, dim), F32)],
        in_specs=in_specs,
        out_specs=[pl.BlockSpec((tokens, dim), corner), pl.BlockSpec((8, dim), lambda i: (i, 0))],
        scratch_shapes=[pltpu.VMEM((tokens, dim), F32)],
        compiler_params=PARAMS,
        name='hidden',
    )(*args)


PLAN = (
    ('de_par', 0), ('dx_send', 0), ('dx_send', 1), ('dx_keep', 0), ('de_par', 1), ('dx_keep', 1),
    ('sum_two', 0), ('de_own', 0), ('sum_two', 1), ('de_own', 1), ('finish', 0), ('finish', 1),
)


def block_lists():
    span = lambda a, n: list(range(a, a + n))
    team = len(RELATIVE)
    halves = lambda b: [sum((span((g * GROUP + k) * team + b, team // 2) for k in range(GROUP)), []) for g in range(CHUNKS // GROUP)]
    lists = [span(k * team, team) for k in range(CHUNKS)]
    lists += [span(g * GROUP * team, GROUP * team) for g in range(CHUNKS // GROUP)]
    return lists + [span(0, CHUNKS * team)] + halves(team // 2) + halves(0)


def solution(mesh):
    shards = mesh.shape['fsdp']
    team = shards // 2
    teams = [list(range(team)), list(range(team, shards))]

    def local(hidden, targets, resp_mask, resp_id, old_logp, ref_logp, rewards, prompt_id, norm_w, embedding):
        tok_dev, dim = hidden.shape
        rows = embedding.shape[0]
        prompts = rewards.shape[0] * shards // GROUP_SIZE
        resp = rewards.shape[0]
        me = lax.axis_index('fsdp')
        wide = tok_dev // CHUNKS
        total = team * tok_dev

        def trade(value, bit):
            return lax.ppermute(value, 'fsdp', [(i, i ^ bit) for i in range(shards)])

        mask_f = resp_mask.astype(F32)
        spots = jnp.arange(tok_dev, dtype=jnp.int32)
        before = jnp.cumsum(resp_mask)
        spot = jnp.where(resp_mask > 0, before - 1, before[-1] + spots - before)
        to_spot = (spots[:, None] == spot[None, :]).astype(BF16)
        rows_first = jnp.dot(to_spot, hidden, preferred_element_type=F32).astype(BF16)
        hid_chunks = [lax.all_gather(rows_first[k * wide:(k + 1) * wide], 'fsdp', axis_index_groups=teams, tiled=True) for k in range(CHUNKS)]

        raw = jnp.stack([targets.astype(F32), mask_f, old_logp, ref_logp, resp_id.astype(F32)])
        raw = lax.dot_general(raw, to_spot.astype(F32), BOTH_LAST, precision=lax.Precision.HIGHEST)
        lanes = lambda v: jnp.pad(v, (0, -v.size % 128)).reshape(-1, 128)
        few = jnp.concatenate([rewards, prompt_id.astype(F32), jnp.sum(mask_f)[None]])
        small = jnp.concatenate([lanes(raw[0]), lanes(few), lanes(norm_w.astype(F32))])
        small = jnp.pad(small, ((0, -small.shape[0] % 8), (0, 0)))
        every = share_call(small, shards, 1)
        emb_later, every = lax.optimization_barrier((embedding, every))
        emb_par = trade(emb_later, team)
        tgt_rows = tok_dev // 128
        rew_all = every[:, tgt_rows, :resp].reshape(-1)
        prompt_all = every[:, tgt_rows, resp:2 * resp].reshape(-1).astype(jnp.int32)
        counts = every[:, tgt_rows, 2 * resp]
        count = jnp.sum(counts)
        gain = every[:, tgt_rows + 1, :norm_w.shape[0]].reshape(-1)
        in_all = (prompt_all[None, :] == jnp.arange(prompts, dtype=jnp.int32)[:, None]).astype(F32)
        totals = jnp.sum(in_all[None] * jnp.stack([rew_all, rew_all * rew_all, jnp.ones_like(rew_all)])[:, None, :], axis=2)
        mean_r = totals[0] / totals[2]
        std_r = jnp.sqrt(jnp.maximum(totals[1] / totals[2] - mean_r * mean_r, 0.0))
        in_own = (prompt_id[None, :] == jnp.arange(prompts, dtype=jnp.int32)[:, None]).astype(F32)
        pick = lambda v: jnp.sum(in_own * v[:, None], axis=0)
        adv_resp = (rewards - pick(mean_r)) / (pick(std_r) + EPSILON)
        adv_tok = jnp.sum(jnp.where(raw[4][None, :] == jnp.arange(resp, dtype=F32)[:, None], adv_resp[:, None], 0.0), axis=0)
        token = jnp.stack([raw[1], raw[2], raw[3], adv_tok, jnp.full_like(mask_f, count)])
        token = jnp.concatenate([token, jnp.zeros((3, tok_dev), F32)])

        in_team = me % team
        place = jnp.bitwise_xor(in_team, jnp.array(RELATIVE, jnp.int32)).astype(jnp.int32)
        tgt_all = every[me - in_team + place, :tgt_rows, :].reshape(team, CHUNKS, wide).transpose(1, 0, 2).reshape(1, total)
        tgt8 = jnp.broadcast_to(tgt_all.astype(jnp.int32), (8, total))
        gain8 = jnp.broadcast_to(gain[None, :], (8, dim))

        active = (counts[me - in_team + place][None, :] > wide * jnp.arange(CHUNKS, dtype=F32)[:, None]).reshape(-1)
        lists = block_lists()
        ids = jnp.array([ids + [0] * (LIST - len(ids)) for ids in lists], jnp.int32)
        used = jnp.array([[1] * len(ids) + [0] * (LIST - len(ids)) for ids in lists], jnp.int32)
        every_id = jnp.arange(LIST, dtype=jnp.int32)
        live = used * jnp.sum((ids[:, :, None] == every_id) * active[None, None, :].astype(jnp.int32), axis=2)
        upto = jnp.sum(live[:, None, :] * (every_id[None, :] <= every_id[:, None]), axis=2)
        n_live = jnp.sum(live, axis=1)
        packed = jnp.minimum(every_id[None, :], n_live[:, None] - 1)
        want = jnp.where(every_id[:N_LISTS, None] < N_LISTS - 4, packed, jnp.maximum(upto - 1, 0))
        chosen = jnp.sum(ids[:, None, :] * live[:, None, :] * (upto[:, None, :] - 1 == want[:, :, None]), axis=2)
        chosen = jnp.where(n_live[:, None] == 0, ids[:, :1], chosen)
        firsts = jnp.stack([me, (me + team) % shards]) * rows
        tab = jnp.concatenate([chosen.reshape(-1), active.astype(jnp.int32), n_live, place, firsts]).astype(jnp.int32)

        stat_own, stat_par, prev, prev_par = [], [], [], []
        order = turned_own = turn_call(embedding, gain8)

        def own(k):
            x_all, z_own, stat = logits_call(tab, 0, embedding, None, tgt8, prev, order, k, k * team, team, wide, hid_chunks[k], gain8)
            prev[:] = [x_all, z_own]
            stat_own.append(stat)
            return stat

        def par(g):
            z, stat = logits_call(tab, 1, emb_par, prev[0], tgt8, prev_par, order, CHUNKS + g, g * GROUP * team, GROUP * team, wide)
            prev_par[:] = [z]
            stat_par.append(stat)
            return stat

        for k in range(CHUNKS - 1):
            order = own(k)
        order = turned_par = turn_call(emb_par, order)
        order = par(0)
        order = own(CHUNKS - 1)
        order = par(1)
        x_all, z_own = prev
        z_par = prev_par[0]
        meta, loss_own = coef_call(stat_own, stat_par, token, tgt8, team, wide, 2)

        state = {}
        order = meta

        def dx_send(k):
            first_block = k * GROUP * team + team // 2
            out = dx_call(tab, z_own, z_par, turned_own, turned_par, meta, order, N_LISTS - 4 + k, first_block, GROUP * team // 2, wide)
            state[k] = trade(out, 1)
            return out

        def dx_keep(k):
            outs = dx_call(tab, z_own, z_par, turned_own, turned_par, meta, order, N_LISTS - 2 + k, k * GROUP * team, GROUP * team // 2, wide, state[k])
            keep_a, send_a, keep_b, send_b = outs
            state[k] = (keep_a, trade(send_a, 2), keep_b, trade(send_b, 4))
            return keep_a

        def sum_two(k):
            fa, sa, fb, sb = second_sum(*state[k], order)
            state[k] = (fa, trade(sa, 4), fb, trade(sb, 2))
            return fa

        def finish(k):
            out, part = hidden_call(state[k], rows_first, gain8, to_spot, state.get('dh'), order, k)
            state['dh'] = out
            state['dg'] = state.get('dg', []) + [part]
            return part

        def de_par(p):
            out = de_call(tab, 1, z_par, x_all, meta, order, CHUNKS + GROUP, p, 2, wide)
            state['ship', p] = trade(out, team)
            return out

        def de_own(p):
            state['de'] = de_call(tab, 0, z_own, x_all, meta, order, CHUNKS + GROUP, p, 2, wide, state['ship', p], state.get('de'))
            return state['de']

        steps = {'de_par': de_par, 'dx_send': dx_send, 'dx_keep': dx_keep, 'sum_two': sum_two, 'de_own': de_own, 'finish': finish}
        for name, arg in PLAN:
            order = steps[name](arg)
        d_hidden = state['dh']
        d_embedding = state['de']
        gain_sum = jnp.sum(jnp.concatenate(state['dg'], axis=0)[::8], axis=0)
        last = jnp.concatenate([gain_sum.reshape(-1, 128), lanes(jnp.sum(loss_own[0])[None])])
        last = jnp.pad(last, ((0, -last.shape[0] % 8), (0, 0)))
        last = jnp.sum(share_call(last, shards, 3), axis=0)
        d_norm_w = lax.dynamic_slice(last.reshape(-1), (me * norm_w.shape[0],), (norm_w.shape[0],))
        mean_loss = last[dim // 128, 0] / count
        return mean_loss, d_hidden, d_embedding, d_norm_w

    tok_spec = P('fsdp')
    row_spec = P('fsdp', None)
    return jax.shard_map(local, mesh=mesh, in_specs=(row_spec, tok_spec, tok_spec, tok_spec, tok_spec, tok_spec, tok_spec, tok_spec, tok_spec, row_spec), out_specs=(P(), row_spec, row_spec, tok_spec), check_vma=False)
```

time: 1740 us -> 625 us (0.36)
  matrix products: 697 us -> 6.82 us
  waiting for transfers between devices: 810 us -> 123 us
  Pallas kernels: 0 us -> 417 us
  blocking collectives: 101 us -> 0 us
  other arithmetic: 93.7 us -> 15.7 us
  starting transfers between devices: 0.08 us -> 26.1 us
    dot_general x12 -> x2, matrix products: 697 us -> 6.82 us  [the longest x1 4.87 us: local(): jnp.dot(to_spot, hidden, preferred_element_type=F32).astype(BF16)]
    unnamed x3 -> x4, waiting for transfers between devices: 633 us -> 1.92 us
    pallas_call x0 -> x23, Pallas kernels: none -> 417 us  [the longest x6 117 us: logits_call(): pl.pallas_call(body, out_shape=out_shape, grid_spec=pltpu.PrefetchScalarG...]
    all_gather x1 -> x4, waiting for transfers between devices: 177 us -> 31.1 us  [local(): lax.all_gather(rows_first[k * wide:(k + 1) * wide], 'fsdp', axis_index_gr...]
    ppermute x0 -> x13, waiting for transfers between devices: none -> 89.6 us  [trade(): return lax.ppermute(value, 'fsdp', [(i, i ^ bit) for i in range(shards)])]
    reduce_sum x12, other arithmetic: 77.3 us -> 6.14 us  [the longest x1 1.72 us: local(): count = jnp.sum(counts)]
    psum x2 -> x0, blocking collectives: 67.6 us -> none  [the longest x1 35.5 us: local(): lax.psum(jax.ops.segment_sum(rew_stats, prompt_id, num_segments=prompts),...]
    unnamed x1 -> x0, blocking collectives: 33.9 us -> none
  transfers between devices with their start and end apart: 2 -> 17, of which waited for: 2 -> 7; matrix products, arithmetic and copies ran while one was open for 2% -> 3% of each run, Pallas kernels for 0% -> 49%
where the time goes in v1:
time: 625 us; the launch traced here: 619 us
  Pallas kernels  417 us (67%)
  waiting for transfers between devices  123 us (20%)
  starting transfers between devices  26.1 us (4%)
  between operations  17 us (3%)
  other arithmetic  15.7 us (3%)
  local copies, waits for them, and re-layouts  13.9 us (2%)
  matrix products  6.82 us (1%)
    pallas_call x6, Pallas kernels, logits_call(): pl.pallas_call(body, out_shape=out_shape, grid_spec=pltpu.PrefetchScalarG...  117 us
    pallas_call x4, Pallas kernels, dx_call(): pl.pallas_call(body, out_shape=out_shape, grid_spec=pltpu.PrefetchScalarG...  111 us
    pallas_call x4, Pallas kernels, de_call(): pl.pallas_call(body, out_shape=jax.ShapeDtypeStruct((rows_all if whole el...  109 us
    ppermute x13, waiting for transfers between devices, trade(): return lax.ppermute(value, 'fsdp', [(i, i ^ bit) for i in range(shards)])  89.6 us
    all_gather x4, waiting for transfers between devices, local(): lax.all_gather(rows_first[k * wide:(k + 1) * wide], 'fsdp', axis_index_gr...  31.1 us
    ppermute x13, starting transfers between devices, trade(): return lax.ppermute(value, 'fsdp', [(i, i ^ bit) for i in range(shards)])  26 us
    pallas_call x2, Pallas kernels, share_call(): pl.pallas_call(body, out_shape=jax.ShapeDtypeStruct((shards,) + block.sha...  19.9 us
    pallas_call x2, Pallas kernels, hidden_call(): pl.pallas_call(body, grid=(n,), out_shape=[jax.ShapeDtypeStruct(hidden.sh...  17.7 us
  transfers between devices with their start and end apart: 17, of which 7 were waited for; matrix products, arithmetic and copies ran while one was open for 3% of the time, Pallas kernels for 49%

profile of v1, /device:TPU:0, one launch (start us, length us, event | category | flops | bytes accessed | tf_op | source)
XLA Modules:
  0.0 619.0 jit_solution(5551523534485418899)
XLA Ops:
  24.5 11.0 %share.2 = f32[16,16,128]{2,1,0:T(8,128)} custom-call(f32[16,128]{1,0:T(8,128)} %fusion.11.in_ref), custom_call_target="tpu_custom_call" | custom-call | tf_op jit(solution)/shard_map/share/pallas_call | solution.py:314
  58.5 21.2 %logits.6 = (bf16[8192,1152]{1,0:T(8,128)(2,1)}, f32[2000,8192]{1,0:T(8,128)}, f32[8,2048]{1,0:T(8,128)}) custom-call(s32[405]{0:T(512)} %concatenate.23.tab_ref, bf16[2000,1152]{1,0:T(8,128)(2,1)} %emb_ref.9, s32[8,8192]{1,0:T(8,128)} %broadcast_in_dim.52.tgt_ref.refs_7_, bf16[2048,1152]{1,0:T(8,128)(2,1)} %all-gather.11.cloned.1.call-done.src_ref, ...), custom_call_target="tpu_custom_call" | custom-call | tf_op jit(solution)/shard_map/logits/pallas_call | solution.py:111
  79.7 15.0 %all-gather.9.cloned.1.call-done.src_ref = bf16[2048,1152]{1,0:T(8,128)(2,1)} async-done(((bf16[256,1152]{1,0:T(8,128)(2,1)}), bf16[2048,1152]{1,0:T(8,128)(2,1)}) %all-gather.9.cloned.1.call-update) | async-done | bytes 4718608 | tf_op jit(solution)/shard_map/all_gather | solution.py:511
  94.8 21.3 %logits.7 = (bf16[8192,1152]{1,0:T(8,128)(2,1)}, f32[2000,8192]{1,0:T(8,128)}, f32[8,2048]{1,0:T(8,128)}) custom-call(s32[405]{0:T(512)} %concatenate.23.tab_ref, bf16[2000,1152]{1,0:T(8,128)(2,1)} %emb_ref.9, s32[8,8192]{1,0:T(8,128)} %broadcast_in_dim.52.tgt_ref.refs_7_, ...), custom_call_target="tpu_custom_call", output_to_operand_aliasing={{0}: (6, {}), {1}: (7, {})} | custom-call | tf_op jit(solution)/shard_map/logits/pallas_call | solution.py:111
  116.1 15.6 %all-gather.7.cloned.1.call-done.src_ref = bf16[2048,1152]{1,0:T(8,128)(2,1)} async-done(((bf16[256,1152]{1,0:T(8,128)(2,1)}), bf16[2048,1152]{1,0:T(8,128)(2,1)}) %all-gather.7.cloned.1.call-update) | async-done | bytes 4718608 | tf_op jit(solution)/shard_map/all_gather | solution.py:511
  131.7 17.3 %logits.8 = (bf16[8192,1152]{1,0:T(8,128)(2,1)}, f32[2000,8192]{1,0:T(8,128)}, f32[8,2048]{1,0:T(8,128)}) custom-call(s32[405]{0:T(512)} %concatenate.23.tab_ref, bf16[2000,1152]{1,0:T(8,128)(2,1)} %emb_ref.9, s32[8,8192]{1,0:T(8,128)} %broadcast_in_dim.52.tgt_ref.refs_7_, ...), custom_call_target="tpu_custom_call", output_to_operand_aliasing={{0}: (6, {}), {1}: (7, {})} | custom-call | tf_op jit(solution)/shard_map/logits/pallas_call | solution.py:111
  156.7 32.6 %logits.9 = (f32[2000,8192]{1,0:T(8,128)}, f32[8,4096]{1,0:T(8,128)}) custom-call(s32[405]{0:T(512)} %concatenate.23.tab_ref, bf16[2000,1152]{1,0:T(8,128)(2,1)} %collective-permute-done.emb_ref, s32[8,8192]{1,0:T(8,128)} %broadcast_in_dim.52.tgt_ref.refs_7_, bf16[8192,1152]{1,0:T(8,128)(2,1)} %get-tuple-element.52.src_ref.refs_2_, ...), custom_call_target="tpu_custom_call" | custom-call | tf_op jit(solution)/shard_map/logits/pallas_call | solution.py:111
  196.7 17.4 %logits.11 = (f32[2000,8192]{1,0:T(8,128)}, f32[8,4096]{1,0:T(8,128)}) custom-call(s32[405]{0:T(512)} %concatenate.23.tab_ref, bf16[2000,1152]{1,0:T(8,128)(2,1)} %collective-permute-done.emb_ref, s32[8,8192]{1,0:T(8,128)} %broadcast_in_dim.52.tgt_ref.refs_7_, ...), custom_call_target="tpu_custom_call", output_to_operand_aliasing={{0}: (5, {})} | custom-call | tf_op jit(solution)/shard_map/logits/pallas_call | solution.py:111
  214.1 13.8 %coef.1 = (f32[8,8192]{1,0:T(8,128)}, f32[8,1024]{1,0:T(8,128)}) custom-call(f32[8,2048]{1,0:T(8,128)} %get-tuple-element.46.refs_1_.refs_0_, f32[8,2048]{1,0:T(8,128)} %get-tuple-element.49.refs_1_, f32[8,2048]{1,0:T(8,128)} %get-tuple-element.53.order_ref.refs_2_, f32[8,2048]{1,0:T(8,128)} %get-tuple-element.58.refs_0_.refs_3_, ...), custom_call_target="tpu_custom_call" | custom-call | tf_op jit(solution)/shard_map/coef/pallas_call | solution.py:389
  227.9 26.5 %de.4.refs_0_ = f32[1000,1152]{1,0:T(8,128)} custom-call(s32[405]{0:T(512)} %concatenate.23.tab_ref, f32[2000,8192]{1,0:T(8,128)} %get-tuple-element.60.refs_0_.refs_1_.zp_ref, f32[2000,8192]{1,0:T(8,128)} %get-tuple-element.60.refs_0_.refs_1_.zp_ref, bf16[8192,1152]{1,0:T(8,128)(2,1)} %get-tuple-element.57.src_ref.refs_2_.refs_3_, ...), custom_call_target="tpu_custom_call" | custom-call | tf_op jit(solution)/shard_map/de/pallas_call | solution.py:251
  254.3 30.6 %dx.4.refs_0_ = f32[8,1152,256]{2,1,0:T(8,128)} custom-call(s32[405]{0:T(512)} %concatenate.23.tab_ref, f32[2000,8192]{1,0:T(8,128)} %get-tuple-element.56.zo_ref.refs_0_.refs_1_, f32[2000,8192]{1,0:T(8,128)} %get-tuple-element.60.refs_0_.refs_1_.zp_ref, bf16[1152,2048]{1,0:T(8,128)(2,1)} %turn.2.refs_1_.eto_ref, bf16[1152,2048]{1,0:T(8,128)(2,1)} %turn.3.refs_0_.etp_ref, ...), custom_call_target="tpu_custom_call" | custom-call | tf_op jit(solution)/shard_map/dx/pallas_call | solution.py:191
  285.0 18.1 %dx.5.refs_0_ = f32[8,1152,256]{2,1,0:T(8,128)} custom-call(s32[405]{0:T(512)} %concatenate.23.tab_ref, f32[2000,8192]{1,0:T(8,128)} %get-tuple-element.56.zo_ref.refs_0_.refs_1_, f32[2000,8192]{1,0:T(8,128)} %get-tuple-element.60.refs_0_.refs_1_.zp_ref, bf16[1152,2048]{1,0:T(8,128)(2,1)} %turn.2.refs_1_.eto_ref, bf16[1152,2048]{1,0:T(8,128)(2,1)} %turn.3.refs_0_.etp_ref, ...), custom_call_target="tpu_custom_call" | custom-call | tf_op jit(solution)/shard_map/dx/pallas_call | solution.py:191
  303.1 8.4 %collective-permute-start.4 = (f32[8,1152,256]{2,1,0:T(8,128)}, f32[8,1152,256]{2,1,0:T(8,128)}, u32[]{:S(2)}, u32[]{:S(2)}) collective-permute-start(f32[8,1152,256]{2,1,0:T(8,128)} %dx.5.refs_0_), channel_id=1, source_target_pairs={{0,1},{1,0},{2,3},{3,2},{4,5},{5,4},{6,7},{7,6},{8,9},{9,8},{10,11... | collective-permute-start | bytes 28311560 | tf_op jit(solution)/shard_map/ppermute | solution.py:503
  311.5 33.3 %dx.6 = (f32[4,576,256]{2,1,0:T(8,128)}, f32[4,576,256]{2,1,0:T(8,128)}, f32[4,576,256]{2,1,0:T(8,128)}, f32[4,576,256]{2,1,0:T(8,128)}) custom-call(s32[405]{0:T(512)} %concatenate.23.tab_ref, f32[2000,8192]{1,0:T(8,128)} %get-tuple-element.56.zo_ref.refs_0_.refs_1_, f32[2000,8192]{1,0:T(8,128)} %get-tuple-element.60.refs_0_.refs_1_.zp_ref, ...), custom_call_target="tpu_custom_call" | custom-call | tf_op jit(solution)/shard_map/dx/pallas_call | solution.py:191
  351.6 26.5 %de.5.refs_0_ = f32[1000,1152]{1,0:T(8,128)} custom-call(s32[405]{0:T(512)} %concatenate.23.tab_ref, f32[2000,8192]{1,0:T(8,128)} %get-tuple-element.60.refs_0_.refs_1_.zp_ref, f32[2000,8192]{1,0:T(8,128)} %get-tuple-element.60.refs_0_.refs_1_.zp_ref, bf16[8192,1152]{1,0:T(8,128)(2,1)} %get-tuple-element.57.src_ref.refs_2_.refs_3_, ...), custom_call_target="tpu_custom_call" | custom-call | tf_op jit(solution)/shard_map/de/pallas_call | solution.py:251
  380.8 29.0 %dx.7 = (f32[4,576,256]{2,1,0:T(8,128)}, f32[4,576,256]{2,1,0:T(8,128)}, f32[4,576,256]{2,1,0:T(8,128)}, f32[4,576,256]{2,1,0:T(8,128)}) custom-call(s32[405]{0:T(512)} %concatenate.23.tab_ref, f32[2000,8192]{1,0:T(8,128)} %get-tuple-element.56.zo_ref.refs_0_.refs_1_, f32[2000,8192]{1,0:T(8,128)} %get-tuple-element.60.refs_0_.refs_1_.zp_ref, ...), custom_call_target="tpu_custom_call" | custom-call | tf_op jit(solution)/shard_map/dx/pallas_call | solution.py:191
  410.0 23.1 %collective-permute-done.3.rb = f32[4,576,256]{2,1,0:T(8,128)} collective-permute-done((f32[4,576,256]{2,1,0:T(8,128)}, f32[4,576,256]{2,1,0:T(8,128)}, u32[]{:S(2)}, u32[]{:S(2)}) %collective-permute-start.3) | collective-permute-done | bytes 2359328 | tf_op jit(solution)/shard_map/ppermute | solution.py:503
  441.3 10.9 %collective-permute-done.9.refs_7_ = f32[1000,1152]{1,0:T(8,128)} collective-permute-done((f32[1000,1152]{1,0:T(8,128)}, f32[1000,1152]{1,0:T(8,128)}, u32[]{:S(2)}, u32[]{:S(2)}) %collective-permute-start.9) | collective-permute-done | bytes 4608032 | tf_op jit(solution)/shard_map/ppermute | solution.py:503
  454.2 28.2 %de.6.order_ref.refs_8_ = f32[2000,1152]{1,0:T(8,128)} custom-call(s32[405]{0:T(512)} %concatenate.23.tab_ref, f32[2000,8192]{1,0:T(8,128)} %get-tuple-element.56.zo_ref.refs_0_.refs_1_, f32[2000,8192]{1,0:T(8,128)} %get-tuple-element.56.zo_ref.refs_0_.refs_1_, bf16[8192,1152]{1,0:T(8,128)(2,1)} %get-tuple-element.57.src_ref.refs_2_.refs_3_, ...), custom_call_target="tpu_custom_call" | custom-call | tf_op jit(solution)/shard_map/de/pallas_call | solution.py:251
  496.2 54.1 %collective-permute-done.10.refs_7_ = f32[1000,1152]{1,0:T(8,128)} collective-permute-done((f32[1000,1152]{1,0:T(8,128)}, f32[1000,1152]{1,0:T(8,128)}, u32[]{:S(2)}, u32[]{:S(2)}) %collective-permute-start.10) | collective-permute-done | bytes 4608032 | tf_op jit(solution)/shard_map/ppermute | solution.py:503
  550.3 28.2 %de.7.refs_7_ = f32[2000,1152]{1,0:T(8,128)} custom-call(s32[405]{0:T(512)} %concatenate.23.tab_ref, f32[2000,8192]{1,0:T(8,128)} %get-tuple-element.56.zo_ref.refs_0_.refs_1_, f32[2000,8192]{1,0:T(8,128)} %get-tuple-element.56.zo_ref.refs_0_.refs_1_, bf16[8192,1152]{1,0:T(8,128)(2,1)} %get-tuple-element.57.src_ref.refs_2_.refs_3_, ...), custom_call_target="tpu_custom_call", output_to_operand_aliasing={{}: (9, {})} | custom-call | tf_op jit(solution)/shard_map/de/pallas_call | solution.py:251
  579.5 8.5 %hidden.2 = (bf16[1024,1152]{1,0:T(8,128)(2,1)}, f32[16,1152]{1,0:T(8,128)}) custom-call(f32[2,576,256]{2,1,0:T(8,128)} %get-tuple-element.68.refs_6_.refs_0_, f32[2,576,256]{2,1,0:T(8,128)} %copy-done.1, f32[2,576,256]{2,1,0:T(8,128)} %get-tuple-element.70.refs_2_, f32[2,576,256]{2,1,0:T(8,128)} %collective-permute-done.6.refs_3_, ...), custom_call_target="tpu_custom_call" | custom-call | tf_op jit(solution)/shard_map/hidden/pallas_call | solution.py:461
  588.1 9.2 %hidden.3 = (bf16[1024,1152]{1,0:T(8,128)(2,1)}, f32[16,1152]{1,0:T(8,128)}) custom-call(f32[2,576,256]{2,1,0:T(8,128)} %get-tuple-element.75.refs_6_.refs_0_, f32[2,576,256]{2,1,0:T(8,128)} %collective-permute-done.11.refs_1_, f32[2,576,256]{2,1,0:T(8,128)} %get-tuple-element.78.refs_2_, f32[2,576,256]{2,1,0:T(8,128)} %collective-permute-done.12.refs_3_, ...), custom_call_target="tpu_custom_call" | custom-call | tf_op jit(solution)/shard_map/hidden/pallas_call | solution.py:461
  598.8 8.9 %share.3 = f32[16,16,128]{2,1,0:T(8,128)} custom-call(f32[16,128]{1,0:T(8,128)} %select_maximum_fusion.in_ref), custom_call_target="tpu_custom_call" | custom-call | tf_op jit(solution)/shard_map/share/pallas_call | solution.py:314
  (150 shorter events, 93.4 us)
Async XLA Ops:
  7.2 50.7 %all-gather.11.cloned.1.call-start = ((), (), s32[]{:S(2)}) async-start(), calls=%async_computation.3 | async-start | bytes 5308416 | tf_op jit(solution)/shard_map/all_gather | solution.py:511
  10.5 11.5 %copy-start.5 = (s32[1024]{0:T(1024)}, s32[1024]{0:T(1024)S(1)}, u32[]{:S(2)}) copy-start(s32[1024]{0:T(1024)S(1)} %get-tuple-element.103) | copy-start | bytes 12292
  16.9 21.4 %copy-start.15 = (s32[8]{0:T(128)S(1)}, s32[8]{0:T(128)}, u32[]{:S(2)}) copy-start(s32[8]{0:T(128)} %constant.76.clone) | copy-start | bytes 100
  16.9 24.7 %copy-start.4 = (s32[11,32]{1,0:T(8,128)S(1)}, s32[11,32]{1,0:T(8,128)}, u32[]{:S(2)}) copy-start(s32[11,32]{1,0:T(8,128)} %constant.77.clone) | copy-start | bytes 4228
  16.9 25.0 %copy-start.7 = (s32[11,32]{1,0:T(8,128)S(1)}, s32[11,32]{1,0:T(8,128)}, u32[]{:S(2)}) copy-start(s32[11,32]{1,0:T(8,128)} %constant.78.clone) | copy-start | bytes 4228
  16.9 25.9 %copy-start.14 = (s32[11]{0:T(128)S(1)}, s32[11]{0:T(128)}, u32[]{:S(2)}) copy-start(s32[11]{0:T(128)} %constant.95) | copy-start | bytes 136
  18.4 76.3 %all-gather.9.cloned.1.call-start = ((), (), s32[]{:S(2)}) async-start(), calls=%async_computation.2 | async-start | bytes 5308416 | tf_op jit(solution)/shard_map/all_gather | solution.py:511
  19.2 112.5 %all-gather.7.cloned.1.call-start = ((), (), s32[]{:S(2)}) async-start(), calls=%async_computation.1 | async-start | bytes 5308416 | tf_op jit(solution)/shard_map/all_gather | solution.py:511
  19.9 169.3 %all-gather.5.cloned.1.call-start = ((), (), s32[]{:S(2)}) async-start(), calls=%async_computation | async-start | bytes 5308416 | tf_op jit(solution)/shard_map/all_gather | solution.py:511
  35.6 113.4 %collective-permute-start = (bf16[2000,1152]{1,0:T(8,128)(2,1)}, bf16[2000,1152]{1,0:T(8,128)(2,1)}, u32[]{:S(2)}, u32[]{:S(2)}) collective-permute-start(bf16[2000,1152]{1,0:T(8,128)(2,1)} %emb_ref.9), channel_id=1, source_target_pairs={{0,8},{1,9},{2,10},{3,11},{4,12},{5,13},{6,14},{7,15},{8,0},{9,1},... | collective-permute-start | bytes 13824008 | tf_op jit(solution)/shard_map/ppermute | solution.py:503
  284.9 26.5 %collective-permute-start.1 = (f32[8,1152,256]{2,1,0:T(8,128)}, f32[8,1152,256]{2,1,0:T(8,128)}, u32[]{:S(2)}, u32[]{:S(2)}) collective-permute-start(f32[8,1152,256]{2,1,0:T(8,128)} %dx.4.refs_0_), channel_id=1, source_target_pairs={{0,1},{1,0},{2,3},{3,2},{4,5},{5,4},{6,7},{7,6},{8,9},{9,8},{10,11... | collective-permute-start | bytes 28311560 | tf_op jit(solution)/shard_map/ppermute | solution.py:503
  303.1 77.7 %collective-permute-start.4 = (f32[8,1152,256]{2,1,0:T(8,128)}, f32[8,1152,256]{2,1,0:T(8,128)}, u32[]{:S(2)}, u32[]{:S(2)}) collective-permute-start(f32[8,1152,256]{2,1,0:T(8,128)} %dx.5.refs_0_), channel_id=1, source_target_pairs={{0,1},{1,0},{2,3},{3,2},{4,5},{5,4},{6,7},{7,6},{8,9},{9,8},{10,11... | collective-permute-start | bytes 28311560 | tf_op jit(solution)/shard_map/ppermute | solution.py:503
  344.8 64.9 %collective-permute-start.2 = (f32[4,576,256]{2,1,0:T(8,128)}, f32[4,576,256]{2,1,0:T(8,128)}, u32[]{:S(2)}, u32[]{:S(2)}) collective-permute-start(f32[4,576,256]{2,1,0:T(8,128)} %get-tuple-element.64), channel_id=1, source_target_pairs={{0,2},{1,3},{2,0},{3,1},{4,6},{5,7},{6,4},{7,5},{8,10},{9,11},{10,... | collective-permute-start | bytes 7077896 | tf_op jit(solution)/shard_map/ppermute | solution.py:503
  345.8 106.4 %collective-permute-start.9 = (f32[1000,1152]{1,0:T(8,128)}, f32[1000,1152]{1,0:T(8,128)}, u32[]{:S(2)}, u32[]{:S(2)}) collective-permute-start(f32[1000,1152]{1,0:T(8,128)} %de.4.refs_0_), channel_id=1, source_target_pairs={{0,8},{1,9},{2,10},{3,11},{4,12},{5,13},{6,14},{7,15},{8,0},{9,1},... | collective-permute-start | bytes 13824008 | tf_op jit(solution)/shard_map/ppermute | solution.py:503
  378.1 172.2 %collective-permute-start.10 = (f32[1000,1152]{1,0:T(8,128)}, f32[1000,1152]{1,0:T(8,128)}, u32[]{:S(2)}, u32[]{:S(2)}) collective-permute-start(f32[1000,1152]{1,0:T(8,128)} %de.5.refs_0_), channel_id=1, source_target_pairs={{0,8},{1,9},{2,10},{3,11},{4,12},{5,13},{6,14},{7,15},{8,0},{9,1},... | collective-permute-start | bytes 13824008 | tf_op jit(solution)/shard_map/ppermute | solution.py:503
  378.1 55.0 %collective-permute-start.3 = (f32[4,576,256]{2,1,0:T(8,128)}, f32[4,576,256]{2,1,0:T(8,128)}, u32[]{:S(2)}, u32[]{:S(2)}) collective-permute-start(f32[4,576,256]{2,1,0:T(8,128)} %get-tuple-element.66), channel_id=1, source_target_pairs={{0,4},{1,5},{2,6},{3,7},{4,0},{5,1},{6,2},{7,3},{8,12},{9,13},{10,... | collective-permute-start | bytes 7077896 | tf_op jit(solution)/shard_map/ppermute | solution.py:503
  409.7 72.6 %collective-permute-start.7 = (f32[4,576,256]{2,1,0:T(8,128)}, f32[4,576,256]{2,1,0:T(8,128)}, u32[]{:S(2)}, u32[]{:S(2)}) collective-permute-start(f32[4,576,256]{2,1,0:T(8,128)} %get-tuple-element.72), channel_id=1, source_target_pairs={{0,2},{1,3},{2,0},{3,1},{4,6},{5,7},{6,4},{7,5},{8,10},{9,11},{10,... | collective-permute-start | bytes 7077896 | tf_op jit(solution)/shard_map/ppermute | solution.py:503
  409.7 74.0 %collective-permute-start.8 = (f32[4,576,256]{2,1,0:T(8,128)}, f32[4,576,256]{2,1,0:T(8,128)}, u32[]{:S(2)}, u32[]{:S(2)}) collective-permute-start(f32[4,576,256]{2,1,0:T(8,128)} %get-tuple-element.74), channel_id=1, source_target_pairs={{0,4},{1,5},{2,6},{3,7},{4,0},{5,1},{6,2},{7,3},{8,12},{9,13},{10,... | collective-permute-start | bytes 7077896 | tf_op jit(solution)/shard_map/ppermute | solution.py:503
  439.3 139.2 %collective-permute-start.5 = (f32[2,576,256]{2,1,0:T(8,128)}, f32[2,576,256]{2,1,0:T(8,128)S(1)}, u32[]{:S(2)}, u32[]{:S(2)}) collective-permute-start(f32[2,576,256]{2,1,0:T(8,128)} %get-tuple-element.69), channel_id=1, source_target_pairs={{0,4},{1,5},{2,6},{3,7},{4,0},{5,1},{6,2},{7,3},{8,12},{9,13},{10,... | collective-permute-start | bytes 3538952 | tf_op jit(solution)/shard_map/ppermute | solution.py:503
  452.2 126.3 %collective-permute-start.6 = (f32[2,576,256]{2,1,0:T(8,128)}, f32[2,576,256]{2,1,0:T(8,128)}, u32[]{:S(2)}, u32[]{:S(2)}) collective-permute-start(f32[2,576,256]{2,1,0:T(8,128)} %get-tuple-element.71), channel_id=1, source_target_pairs={{0,2},{1,3},{2,0},{3,1},{4,6},{5,7},{6,4},{7,5},{8,10},{9,11},{10,... | collective-permute-start | bytes 3538952 | tf_op jit(solution)/shard_map/ppermute | solution.py:503
  483.7 8.2 %copy-start.6 = (s32[1024]{0:T(1024)S(1)}, s32[1024]{0:T(1024)}, u32[]{:S(2)}) copy-start(s32[1024]{0:T(1024)} %copy-done.5) | copy-start | bytes 12292
  489.8 98.2 %collective-permute-start.11 = (f32[2,576,256]{2,1,0:T(8,128)}, f32[2,576,256]{2,1,0:T(8,128)}, u32[]{:S(2)}, u32[]{:S(2)}) collective-permute-start(f32[2,576,256]{2,1,0:T(8,128)} %get-tuple-element.77), channel_id=1, source_target_pairs={{0,4},{1,5},{2,6},{3,7},{4,0},{5,1},{6,2},{7,3},{8,12},{9,13},{10,... | collective-permute-start | bytes 3538952 | tf_op jit(solution)/shard_map/ppermute | solution.py:503
  491.9 96.2 %collective-permute-start.12 = (f32[2,576,256]{2,1,0:T(8,128)}, f32[2,576,256]{2,1,0:T(8,128)}, u32[]{:S(2)}, u32[]{:S(2)}) collective-permute-start(f32[2,576,256]{2,1,0:T(8,128)} %get-tuple-element.79), channel_id=1, source_target_pairs={{0,2},{1,3},{2,0},{3,1},{4,6},{5,7},{6,4},{7,5},{8,10},{9,11},{10,... | collective-permute-start | bytes 3538952 | tf_op jit(solution)/shard_map/ppermute | solution.py:503
  588.1 9.2 %copy-start.2 = (f32[16,1152]{1,0:T(8,128)S(1)}, f32[16,1152]{1,0:T(8,128)}, u32[]{:S(2)}) copy-start(f32[16,1152]{1,0:T(8,128)} %get-tuple-element.76.refs_7_) | copy-start | bytes 221188
  (10 other events, 33.1 us)
Sparse Core Ops, SparseCore 0:
  18.5 39.2 all-gather.10
  59.7 35.0 all-gather.8
  96.6 35.0 all-gather.6
  133.9 35.0 all-gather.4

commit v2 on v1

--- a/solution.py
+++ b/solution.py
@@ -472,7 +472,7 @@
 
 PLAN = (
     ('de_par', 0), ('dx_send', 0), ('dx_send', 1), ('dx_keep', 0), ('de_par', 1), ('dx_keep', 1),
-    ('sum_two', 0), ('de_own', 0), ('sum_two', 1), ('de_own', 1), ('finish', 0), ('finish', 1),
+    ('sum_two', 0), ('de_own', 0), ('de_last', 1), ('sum_two', 1), ('finish', 0), ('add', 1), ('finish', 1),
 )
 
 
@@ -609,15 +609,24 @@
             return part
 
         def de_par(p):
-            out = de_call(tab, 1, z_par, x_all, meta, order, CHUNKS + GROUP, p, 2, wide)
+            out = de_call(tab, 1, z_par, x_all, meta, order, CHUNKS + GROUP, p, GROUP, wide)
             state['ship', p] = trade(out, team)
             return out
 
         def de_own(p):
-            state['de'] = de_call(tab, 0, z_own, x_all, meta, order, CHUNKS + GROUP, p, 2, wide, state['ship', p], state.get('de'))
+            state['de'] = de_call(tab, 0, z_own, x_all, meta, order, CHUNKS + GROUP, p, GROUP, wide, state['ship', p], state.get('de'))
             return state['de']
 
-        steps = {'de_par': de_par, 'dx_send': dx_send, 'dx_keep': dx_keep, 'sum_two': sum_two, 'de_own': de_own, 'finish': finish}
+        def de_last(p):
+            state['last'] = de_call(tab, 0, z_own, x_all, meta, order, CHUNKS + GROUP, p, GROUP, wide)
+            return state['last']
+
+        def add(p):
+            more, _ = lax.optimization_barrier((state['ship', p], order))
+            state['de'] = state['de'].at[rows // GROUP:].set(state['last'] + more)
+            return state['de']
+
+        steps = {'de_last': de_last, 'add': add, 'de_par': de_par, 'dx_send': dx_send, 'dx_keep': dx_keep, 'sum_two': sum_two, 'de_own': de_own, 'finish': finish}
         for name, arg in PLAN:
             order = steps[name](arg)
         d_hidden = state['dh']

time: 625 us -> 570 us (0.912)
  waiting for transfers between devices: 123 us -> 65.1 us
  other arithmetic: 15.7 us -> 22 us
    ppermute x13, waiting for transfers between devices: 89.6 us -> 32.2 us  [trade(): return lax.ppermute(value, 'fsdp', [(i, i ^ bit) for i in range(shards)])]
    scatter x0 -> x1, other arithmetic: none -> 6.31 us  [add(): state['de'] = state['de'].at[rows // GROUP:].set(state['last'] + more)]
  transfers between devices with their start and end apart: 17 -> 17, of which waited for: 7 -> 6; matrix products, arithmetic and copies ran while one was open for 3% -> 5% of each run, Pallas kernels for 49% -> 53%
where the time goes in v2:
time: 570 us; the launch traced here: 563 us
  Pallas kernels  415 us (73%)
  waiting for transfers between devices  65.1 us (11%)
  starting transfers between devices  24 us (4%)
  other arithmetic  22 us (4%)
  between operations  17 us (3%)
  local copies, waits for them, and re-layouts  13.9 us (2%)
  matrix products  6.82 us (1%)
    pallas_call x6, Pallas kernels, logits_call(): pl.pallas_call(body, out_shape=out_shape, grid_spec=pltpu.PrefetchScalarG...  117 us
    pallas_call x4, Pallas kernels, dx_call(): pl.pallas_call(body, out_shape=out_shape, grid_spec=pltpu.PrefetchScalarG...  111 us
    pallas_call x4, Pallas kernels, de_call(): pl.pallas_call(body, out_shape=jax.ShapeDtypeStruct((rows_all if whole el...  108 us
    ppermute x13, waiting for transfers between devices, trade(): return lax.ppermute(value, 'fsdp', [(i, i ^ bit) for i in range(shards)])  32.2 us
    all_gather x4, waiting for transfers between devices, local(): lax.all_gather(rows_first[k * wide:(k + 1) * wide], 'fsdp', axis_index_gr...  31 us
    ppermute x13, starting transfers between devices, trade(): return lax.ppermute(value, 'fsdp', [(i, i ^ bit) for i in range(shards)])  23.8 us
    pallas_call x2, Pallas kernels, share_call(): pl.pallas_call(body, out_shape=jax.ShapeDtypeStruct((shards,) + block.sha...  19.3 us
    pallas_call x2, Pallas kernels, hidden_call(): pl.pallas_call(body, grid=(n,), out_shape=[jax.ShapeDtypeStruct(hidden.sh...  17.7 us
  transfers between devices with their start and end apart: 17, of which 6 were waited for; matrix products, arithmetic and copies ran while one was open for 5% of the time, Pallas kernels for 53%

profile of v2, /device:TPU:0, one launch (start us, length us, event | category | flops | bytes accessed | tf_op | source)
XLA Modules:
  0.0 563.4 jit_solution(1177434413282870475)
XLA Ops:
  24.6 11.0 %share.2 = f32[16,16,128]{2,1,0:T(8,128)} custom-call(f32[16,128]{1,0:T(8,128)} %fusion.11.in_ref), custom_call_target="tpu_custom_call" | custom-call | tf_op jit(solution)/shard_map/share/pallas_call | solution.py:314
  44.6 8.1 %turn.2.refs_1_.eto_ref = bf16[1152,2048]{1,0:T(8,128)(2,1)} custom-call(bf16[2000,1152]{1,0:T(8,128)(2,1)} %emb_ref.9, f32[8,1152]{1,0:T(8,128)} %broadcast_in_dim.54.order_ref.refs_0_.refs_5_), custom_call_target="tpu_custom_call" | custom-call | tf_op jit(solution)/shard_map/turn/pallas_call | solution.py:276
  58.6 21.2 %logits.6 = (bf16[8192,1152]{1,0:T(8,128)(2,1)}, f32[2000,8192]{1,0:T(8,128)}, f32[8,2048]{1,0:T(8,128)}) custom-call(s32[405]{0:T(512)} %concatenate.25.tab_ref, bf16[2000,1152]{1,0:T(8,128)(2,1)} %emb_ref.9, s32[8,8192]{1,0:T(8,128)} %broadcast_in_dim.52.tgt_ref.refs_7_, bf16[2048,1152]{1,0:T(8,128)(2,1)} %all-gather.11.cloned.1.call-done.src_ref, ...), custom_call_target="tpu_custom_call" | custom-call | tf_op jit(solution)/shard_map/logits/pallas_call | solution.py:111
  79.8 15.0 %all-gather.9.cloned.1.call-done.src_ref = bf16[2048,1152]{1,0:T(8,128)(2,1)} async-done(((bf16[256,1152]{1,0:T(8,128)(2,1)}), bf16[2048,1152]{1,0:T(8,128)(2,1)}) %all-gather.9.cloned.1.call-update) | async-done | bytes 4718608 | tf_op jit(solution)/shard_map/all_gather | solution.py:511
  94.7 21.3 %logits.7 = (bf16[8192,1152]{1,0:T(8,128)(2,1)}, f32[2000,8192]{1,0:T(8,128)}, f32[8,2048]{1,0:T(8,128)}) custom-call(s32[405]{0:T(512)} %concatenate.25.tab_ref, bf16[2000,1152]{1,0:T(8,128)(2,1)} %emb_ref.9, s32[8,8192]{1,0:T(8,128)} %broadcast_in_dim.52.tgt_ref.refs_7_, ...), custom_call_target="tpu_custom_call", output_to_operand_aliasing={{0}: (6, {}), {1}: (7, {})} | custom-call | tf_op jit(solution)/shard_map/logits/pallas_call | solution.py:111
  116.0 15.6 %all-gather.7.cloned.1.call-done.src_ref = bf16[2048,1152]{1,0:T(8,128)(2,1)} async-done(((bf16[256,1152]{1,0:T(8,128)(2,1)}), bf16[2048,1152]{1,0:T(8,128)(2,1)}) %all-gather.7.cloned.1.call-update) | async-done | bytes 4718608 | tf_op jit(solution)/shard_map/all_gather | solution.py:511
  131.7 17.3 %logits.8 = (bf16[8192,1152]{1,0:T(8,128)(2,1)}, f32[2000,8192]{1,0:T(8,128)}, f32[8,2048]{1,0:T(8,128)}) custom-call(s32[405]{0:T(512)} %concatenate.25.tab_ref, bf16[2000,1152]{1,0:T(8,128)(2,1)} %emb_ref.9, s32[8,8192]{1,0:T(8,128)} %broadcast_in_dim.52.tgt_ref.refs_7_, ...), custom_call_target="tpu_custom_call", output_to_operand_aliasing={{0}: (6, {}), {1}: (7, {})} | custom-call | tf_op jit(solution)/shard_map/logits/pallas_call | solution.py:111
  156.6 32.6 %logits.9 = (f32[2000,8192]{1,0:T(8,128)}, f32[8,4096]{1,0:T(8,128)}) custom-call(s32[405]{0:T(512)} %concatenate.25.tab_ref, bf16[2000,1152]{1,0:T(8,128)(2,1)} %collective-permute-done.emb_ref, s32[8,8192]{1,0:T(8,128)} %broadcast_in_dim.52.tgt_ref.refs_7_, bf16[8192,1152]{1,0:T(8,128)(2,1)} %get-tuple-element.65.src_ref.refs_2_, ...), custom_call_target="tpu_custom_call" | custom-call | tf_op jit(solution)/shard_map/logits/pallas_call | solution.py:111
  196.7 17.4 %logits.11 = (f32[2000,8192]{1,0:T(8,128)}, f32[8,4096]{1,0:T(8,128)}) custom-call(s32[405]{0:T(512)} %concatenate.25.tab_ref, bf16[2000,1152]{1,0:T(8,128)(2,1)} %collective-permute-done.emb_ref, s32[8,8192]{1,0:T(8,128)} %broadcast_in_dim.52.tgt_ref.refs_7_, ...), custom_call_target="tpu_custom_call", output_to_operand_aliasing={{0}: (5, {})} | custom-call | tf_op jit(solution)/shard_map/logits/pallas_call | solution.py:111
  214.1 13.7 %coef.1 = (f32[8,8192]{1,0:T(8,128)}, f32[8,1024]{1,0:T(8,128)}) custom-call(f32[8,2048]{1,0:T(8,128)} %get-tuple-element.59.refs_1_.refs_0_, f32[8,2048]{1,0:T(8,128)} %get-tuple-element.62.refs_1_, f32[8,2048]{1,0:T(8,128)} %get-tuple-element.66.order_ref.refs_2_, f32[8,2048]{1,0:T(8,128)} %get-tuple-element.71.refs_0_.refs_3_, ...), custom_call_target="tpu_custom_call" | custom-call | tf_op jit(solution)/shard_map/coef/pallas_call | solution.py:389
  227.8 26.5 %de.4.refs_0_ = f32[1000,1152]{1,0:T(8,128)} custom-call(s32[405]{0:T(512)} %concatenate.25.tab_ref, f32[2000,8192]{1,0:T(8,128)} %get-tuple-element.73.refs_0_.refs_1_.zp_ref, f32[2000,8192]{1,0:T(8,128)} %get-tuple-element.73.refs_0_.refs_1_.zp_ref, bf16[8192,1152]{1,0:T(8,128)(2,1)} %get-tuple-element.70.src_ref.refs_2_.refs_3_, ...), custom_call_target="tpu_custom_call" | custom-call | tf_op jit(solution)/shard_map/de/pallas_call | solution.py:251
  254.3 30.6 %dx.4.refs_0_ = f32[8,1152,256]{2,1,0:T(8,128)} custom-call(s32[405]{0:T(512)} %concatenate.25.tab_ref, f32[2000,8192]{1,0:T(8,128)} %get-tuple-element.69.zo_ref.refs_0_.refs_1_, f32[2000,8192]{1,0:T(8,128)} %get-tuple-element.73.refs_0_.refs_1_.zp_ref, bf16[1152,2048]{1,0:T(8,128)(2,1)} %turn.2.refs_1_.eto_ref, bf16[1152,2048]{1,0:T(8,128)(2,1)} %turn.3.refs_0_.etp_ref, ...), custom_call_target="tpu_custom_call" | custom-call | tf_op jit(solution)/shard_map/dx/pallas_call | solution.py:191
  284.9 18.1 %dx.5.refs_0_ = f32[8,1152,256]{2,1,0:T(8,128)} custom-call(s32[405]{0:T(512)} %concatenate.25.tab_ref, f32[2000,8192]{1,0:T(8,128)} %get-tuple-element.69.zo_ref.refs_0_.refs_1_, f32[2000,8192]{1,0:T(8,128)} %get-tuple-element.73.refs_0_.refs_1_.zp_ref, bf16[1152,2048]{1,0:T(8,128)(2,1)} %turn.2.refs_1_.eto_ref, bf16[1152,2048]{1,0:T(8,128)(2,1)} %turn.3.refs_0_.etp_ref, ...), custom_call_target="tpu_custom_call" | custom-call | tf_op jit(solution)/shard_map/dx/pallas_call | solution.py:191
  303.0 8.4 %collective-permute-start.4 = (f32[8,1152,256]{2,1,0:T(8,128)}, f32[8,1152,256]{2,1,0:T(8,128)}, u32[]{:S(2)}, u32[]{:S(2)}) collective-permute-start(f32[8,1152,256]{2,1,0:T(8,128)} %dx.5.refs_0_), channel_id=1, source_target_pairs={{0,1},{1,0},{2,3},{3,2},{4,5},{5,4},{6,7},{7,6},{8,9},{9,8},{10,11... | collective-permute-start | bytes 28311560 | tf_op jit(solution)/shard_map/ppermute | solution.py:503
  318.2 33.3 %dx.6 = (f32[4,576,256]{2,1,0:T(8,128)}, f32[4,576,256]{2,1,0:T(8,128)}, f32[4,576,256]{2,1,0:T(8,128)}, f32[4,576,256]{2,1,0:T(8,128)}) custom-call(s32[405]{0:T(512)} %concatenate.25.tab_ref, f32[2000,8192]{1,0:T(8,128)} %get-tuple-element.69.zo_ref.refs_0_.refs_1_, f32[2000,8192]{1,0:T(8,128)} %get-tuple-element.73.refs_0_.refs_1_.zp_ref, ...), custom_call_target="tpu_custom_call" | custom-call | tf_op jit(solution)/shard_map/dx/pallas_call | solution.py:191
  351.5 26.6 %de.5.refs_0_ = f32[1000,1152]{1,0:T(8,128)} custom-call(s32[405]{0:T(512)} %concatenate.25.tab_ref, f32[2000,8192]{1,0:T(8,128)} %get-tuple-element.73.refs_0_.refs_1_.zp_ref, f32[2000,8192]{1,0:T(8,128)} %get-tuple-element.73.refs_0_.refs_1_.zp_ref, bf16[8192,1152]{1,0:T(8,128)(2,1)} %get-tuple-element.70.src_ref.refs_2_.refs_3_, ...), custom_call_target="tpu_custom_call" | custom-call | tf_op jit(solution)/shard_map/de/pallas_call | solution.py:251
  380.8 29.0 %dx.7 = (f32[4,576,256]{2,1,0:T(8,128)}, f32[4,576,256]{2,1,0:T(8,128)}, f32[4,576,256]{2,1,0:T(8,128)}, f32[4,576,256]{2,1,0:T(8,128)}) custom-call(s32[405]{0:T(512)} %concatenate.25.tab_ref, f32[2000,8192]{1,0:T(8,128)} %get-tuple-element.69.zo_ref.refs_0_.refs_1_, f32[2000,8192]{1,0:T(8,128)} %get-tuple-element.73.refs_0_.refs_1_.zp_ref, ...), custom_call_target="tpu_custom_call" | custom-call | tf_op jit(solution)/shard_map/dx/pallas_call | solution.py:191
  410.1 23.1 %collective-permute-done.3.rb = f32[4,576,256]{2,1,0:T(8,128)} collective-permute-done((f32[4,576,256]{2,1,0:T(8,128)}, f32[4,576,256]{2,1,0:T(8,128)}, u32[]{:S(2)}, u32[]{:S(2)}) %collective-permute-start.3) | collective-permute-done | bytes 2359328 | tf_op jit(solution)/shard_map/ppermute | solution.py:503
  444.9 28.2 %de.6.refs_6_ = f32[2000,1152]{1,0:T(8,128)} custom-call(s32[405]{0:T(512)} %concatenate.25.tab_ref, f32[2000,8192]{1,0:T(8,128)} %get-tuple-element.69.zo_ref.refs_0_.refs_1_, f32[2000,8192]{1,0:T(8,128)} %get-tuple-element.69.zo_ref.refs_0_.refs_1_, bf16[8192,1152]{1,0:T(8,128)(2,1)} %get-tuple-element.70.src_ref.refs_2_.refs_3_, ...), custom_call_target="tpu_custom_call" | custom-call | tf_op jit(solution)/shard_map/de/pallas_call | solution.py:251
  473.1 26.3 %de.7.order_ref = f32[1000,1152]{1,0:T(8,128)} custom-call(s32[405]{0:T(512)} %concatenate.25.tab_ref, f32[2000,8192]{1,0:T(8,128)} %get-tuple-element.69.zo_ref.refs_0_.refs_1_, f32[2000,8192]{1,0:T(8,128)} %get-tuple-element.69.zo_ref.refs_0_.refs_1_, bf16[8192,1152]{1,0:T(8,128)(2,1)} %get-tuple-element.70.src_ref.refs_2_.refs_3_, ...), custom_call_target="tpu_custom_call" | custom-call | tf_op jit(solution)/shard_map/de/pallas_call | solution.py:251
  510.0 8.5 %hidden.2 = (bf16[1024,1152]{1,0:T(8,128)(2,1)}, f32[16,1152]{1,0:T(8,128)}) custom-call(f32[2,576,256]{2,1,0:T(8,128)} %get-tuple-element.81.refs_6_.refs_0_, f32[2,576,256]{2,1,0:T(8,128)} %copy-done.1, f32[2,576,256]{2,1,0:T(8,128)} %get-tuple-element.83.refs_2_, f32[2,576,256]{2,1,0:T(8,128)} %collective-permute-done.6.refs_3_, ...), custom_call_target="tpu_custom_call" | custom-call | tf_op jit(solution)/shard_map/hidden/pallas_call | solution.py:461
  524.8 8.3 %collective-permute-done.10.refs_1_ = f32[2,576,256]{2,1,0:T(8,128)} collective-permute-done((f32[2,576,256]{2,1,0:T(8,128)}, f32[2,576,256]{2,1,0:T(8,128)}, u32[]{:S(2)}, u32[]{:S(2)}) %collective-permute-start.10) | collective-permute-done | bytes 1179680 | tf_op jit(solution)/shard_map/ppermute | solution.py:503
  533.1 9.2 %hidden.3 = (bf16[1024,1152]{1,0:T(8,128)(2,1)}, f32[16,1152]{1,0:T(8,128)}) custom-call(f32[2,576,256]{2,1,0:T(8,128)} %get-tuple-element.88.refs_7_.refs_0_, f32[2,576,256]{2,1,0:T(8,128)} %collective-permute-done.10.refs_1_, f32[2,576,256]{2,1,0:T(8,128)} %get-tuple-element.91.refs_2_, f32[2,576,256]{2,1,0:T(8,128)} %collective-permute-done.11.refs_3_, ...), custom_call_target="tpu_custom_call" | custom-call | tf_op jit(solution)/shard_map/hidden/pallas_call | solution.py:461
  543.8 8.3 %share.3 = f32[16,16,128]{2,1,0:T(8,128)} custom-call(f32[16,128]{1,0:T(8,128)} %select_maximum_fusion.in_ref), custom_call_target="tpu_custom_call" | custom-call | tf_op jit(solution)/shard_map/share/pallas_call | solution.py:314
  (151 shorter events, 88.9 us)
Async XLA Ops:
  7.2 50.7 %all-gather.11.cloned.1.call-start = ((), (), s32[]{:S(2)}) async-start(), calls=%async_computation.3 | async-start | bytes 5308416 | tf_op jit(solution)/shard_map/all_gather | solution.py:511
  10.5 11.5 %copy-start.5 = (s32[1024]{0:T(1024)}, s32[1024]{0:T(1024)S(1)}, u32[]{:S(2)}) copy-start(s32[1024]{0:T(1024)S(1)} %get-tuple-element.117) | copy-start | bytes 12292
  16.9 21.4 %copy-start.15 = (s32[8]{0:T(128)S(1)}, s32[8]{0:T(128)}, u32[]{:S(2)}) copy-start(s32[8]{0:T(128)} %constant.104.clone) | copy-start | bytes 100
  16.9 24.7 %copy-start.4 = (s32[11,32]{1,0:T(8,128)S(1)}, s32[11,32]{1,0:T(8,128)}, u32[]{:S(2)}) copy-start(s32[11,32]{1,0:T(8,128)} %constant.105.clone) | copy-start | bytes 4228
  16.9 25.0 %copy-start.7 = (s32[11,32]{1,0:T(8,128)S(1)}, s32[11,32]{1,0:T(8,128)}, u32[]{:S(2)}) copy-start(s32[11,32]{1,0:T(8,128)} %constant.106.clone) | copy-start | bytes 4228
  16.9 25.9 %copy-start.14 = (s32[11]{0:T(128)S(1)}, s32[11]{0:T(128)}, u32[]{:S(2)}) copy-start(s32[11]{0:T(128)} %constant.123) | copy-start | bytes 136
  18.4 76.3 %all-gather.9.cloned.1.call-start = ((), (), s32[]{:S(2)}) async-start(), calls=%async_computation.2 | async-start | bytes 5308416 | tf_op jit(solution)/shard_map/all_gather | solution.py:511
  19.2 112.5 %all-gather.7.cloned.1.call-start = ((), (), s32[]{:S(2)}) async-start(), calls=%async_computation.1 | async-start | bytes 5308416 | tf_op jit(solution)/shard_map/all_gather | solution.py:511
  19.9 169.3 %all-gather.5.cloned.1.call-start = ((), (), s32[]{:S(2)}) async-start(), calls=%async_computation | async-start | bytes 5308416 | tf_op jit(solution)/shard_map/all_gather | solution.py:511
  35.6 113.4 %collective-permute-start = (bf16[2000,1152]{1,0:T(8,128)(2,1)}, bf16[2000,1152]{1,0:T(8,128)(2,1)}, u32[]{:S(2)}, u32[]{:S(2)}) collective-permute-start(bf16[2000,1152]{1,0:T(8,128)(2,1)} %emb_ref.9), channel_id=1, source_target_pairs={{0,8},{1,9},{2,10},{3,11},{4,12},{5,13},{6,14},{7,15},{8,0},{9,1},... | collective-permute-start | bytes 13824008 | tf_op jit(solution)/shard_map/ppermute | solution.py:503
  284.9 33.3 %collective-permute-start.1 = (f32[8,1152,256]{2,1,0:T(8,128)}, f32[8,1152,256]{2,1,0:T(8,128)}, u32[]{:S(2)}, u32[]{:S(2)}) collective-permute-start(f32[8,1152,256]{2,1,0:T(8,128)} %dx.4.refs_0_), channel_id=1, source_target_pairs={{0,1},{1,0},{2,3},{3,2},{4,5},{5,4},{6,7},{7,6},{8,9},{9,8},{10,11... | collective-permute-start | bytes 28311560 | tf_op jit(solution)/shard_map/ppermute | solution.py:503
  303.0 77.8 %collective-permute-start.4 = (f32[8,1152,256]{2,1,0:T(8,128)}, f32[8,1152,256]{2,1,0:T(8,128)}, u32[]{:S(2)}, u32[]{:S(2)}) collective-permute-start(f32[8,1152,256]{2,1,0:T(8,128)} %dx.5.refs_0_), channel_id=1, source_target_pairs={{0,1},{1,0},{2,3},{3,2},{4,5},{5,4},{6,7},{7,6},{8,9},{9,8},{10,11... | collective-permute-start | bytes 28311560 | tf_op jit(solution)/shard_map/ppermute | solution.py:503
  311.5 129.9 %collective-permute-start.9 = (f32[1000,1152]{1,0:T(8,128)}, f32[1000,1152]{1,0:T(8,128)}, u32[]{:S(2)}, u32[]{:S(2)}) collective-permute-start(f32[1000,1152]{1,0:T(8,128)} %de.4.refs_0_), channel_id=1, source_target_pairs={{0,8},{1,9},{2,10},{3,11},{4,12},{5,13},{6,14},{7,15},{8,0},{9,1},... | collective-permute-start | bytes 13824008 | tf_op jit(solution)/shard_map/ppermute | solution.py:503
  351.5 58.3 %collective-permute-start.2 = (f32[4,576,256]{2,1,0:T(8,128)}, f32[4,576,256]{2,1,0:T(8,128)}, u32[]{:S(2)}, u32[]{:S(2)}) collective-permute-start(f32[4,576,256]{2,1,0:T(8,128)} %get-tuple-element.77), channel_id=1, source_target_pairs={{0,2},{1,3},{2,0},{3,1},{4,6},{5,7},{6,4},{7,5},{8,10},{9,11},{10,... | collective-permute-start | bytes 7077896 | tf_op jit(solution)/shard_map/ppermute | solution.py:503
  378.1 140.4 %collective-permute-start.12 = (f32[1000,1152]{1,0:T(8,128)}, f32[1000,1152]{1,0:T(8,128)}, u32[]{:S(2)}, u32[]{:S(2)}) collective-permute-start(f32[1000,1152]{1,0:T(8,128)} %de.5.refs_0_), channel_id=1, source_target_pairs={{0,8},{1,9},{2,10},{3,11},{4,12},{5,13},{6,14},{7,15},{8,0},{9,1},... | collective-permute-start | bytes 13824008 | tf_op jit(solution)/shard_map/ppermute | solution.py:503
  378.1 55.1 %collective-permute-start.3 = (f32[4,576,256]{2,1,0:T(8,128)}, f32[4,576,256]{2,1,0:T(8,128)}, u32[]{:S(2)}, u32[]{:S(2)}) collective-permute-start(f32[4,576,256]{2,1,0:T(8,128)} %get-tuple-element.79), channel_id=1, source_target_pairs={{0,4},{1,5},{2,6},{3,7},{4,0},{5,1},{6,2},{7,3},{8,12},{9,13},{10,... | collective-permute-start | bytes 7077896 | tf_op jit(solution)/shard_map/ppermute | solution.py:503
  409.8 89.6 %collective-permute-start.7 = (f32[4,576,256]{2,1,0:T(8,128)}, f32[4,576,256]{2,1,0:T(8,128)}, u32[]{:S(2)}, u32[]{:S(2)}) collective-permute-start(f32[4,576,256]{2,1,0:T(8,128)} %get-tuple-element.85), channel_id=1, source_target_pairs={{0,2},{1,3},{2,0},{3,1},{4,6},{5,7},{6,4},{7,5},{8,10},{9,11},{10,... | collective-permute-start | bytes 7077896 | tf_op jit(solution)/shard_map/ppermute | solution.py:503
  409.8 89.6 %collective-permute-start.8 = (f32[4,576,256]{2,1,0:T(8,128)}, f32[4,576,256]{2,1,0:T(8,128)}, u32[]{:S(2)}, u32[]{:S(2)}) collective-permute-start(f32[4,576,256]{2,1,0:T(8,128)} %get-tuple-element.87), channel_id=1, source_target_pairs={{0,4},{1,5},{2,6},{3,7},{4,0},{5,1},{6,2},{7,3},{8,12},{9,13},{10,... | collective-permute-start | bytes 7077896 | tf_op jit(solution)/shard_map/ppermute | solution.py:503
  433.2 8.2 %copy-start.6 = (s32[1024]{0:T(1024)S(1)}, s32[1024]{0:T(1024)}, u32[]{:S(2)}) copy-start(s32[1024]{0:T(1024)} %copy-done.5) | copy-start | bytes 12292
  439.3 69.6 %collective-permute-start.5 = (f32[2,576,256]{2,1,0:T(8,128)}, f32[2,576,256]{2,1,0:T(8,128)S(1)}, u32[]{:S(2)}, u32[]{:S(2)}) collective-permute-start(f32[2,576,256]{2,1,0:T(8,128)} %get-tuple-element.82), channel_id=1, source_target_pairs={{0,4},{1,5},{2,6},{3,7},{4,0},{5,1},{6,2},{7,3},{8,12},{9,13},{10,... | collective-permute-start | bytes 3538952 | tf_op jit(solution)/shard_map/ppermute | solution.py:503
  441.4 67.6 %collective-permute-start.6 = (f32[2,576,256]{2,1,0:T(8,128)}, f32[2,576,256]{2,1,0:T(8,128)}, u32[]{:S(2)}, u32[]{:S(2)}) collective-permute-start(f32[2,576,256]{2,1,0:T(8,128)} %get-tuple-element.84), channel_id=1, source_target_pairs={{0,2},{1,3},{2,0},{3,1},{4,6},{5,7},{6,4},{7,5},{8,10},{9,11},{10,... | collective-permute-start | bytes 3538952 | tf_op jit(solution)/shard_map/ppermute | solution.py:503
  505.6 27.5 %collective-permute-start.10 = (f32[2,576,256]{2,1,0:T(8,128)}, f32[2,576,256]{2,1,0:T(8,128)}, u32[]{:S(2)}, u32[]{:S(2)}) collective-permute-start(f32[2,576,256]{2,1,0:T(8,128)} %get-tuple-element.90), channel_id=1, source_target_pairs={{0,4},{1,5},{2,6},{3,7},{4,0},{5,1},{6,2},{7,3},{8,12},{9,13},{10,... | collective-permute-start | bytes 3538952 | tf_op jit(solution)/shard_map/ppermute | solution.py:503
  506.8 26.3 %collective-permute-start.11 = (f32[2,576,256]{2,1,0:T(8,128)}, f32[2,576,256]{2,1,0:T(8,128)}, u32[]{:S(2)}, u32[]{:S(2)}) collective-permute-start(f32[2,576,256]{2,1,0:T(8,128)} %get-tuple-element.92), channel_id=1, source_target_pairs={{0,2},{1,3},{2,0},{3,1},{4,6},{5,7},{6,4},{7,5},{8,10},{9,11},{10,... | collective-permute-start | bytes 3538952 | tf_op jit(solution)/shard_map/ppermute | solution.py:503
  533.1 9.2 %copy-start.2 = (f32[16,1152]{1,0:T(8,128)S(1)}, f32[16,1152]{1,0:T(8,128)}, u32[]{:S(2)}) copy-start(f32[16,1152]{1,0:T(8,128)} %get-tuple-element.89) | copy-start | bytes 221188
  (10 other events, 33.2 us)
Sparse Core Ops, SparseCore 0:
  18.6 39.2 all-gather.10
  59.7 35.0 all-gather.8
  96.6 35.0 all-gather.6
  133.9 35.0 all-gather.4
